TPU v7x, 32 devices: a whole 2x2x4 slice. The times are simulated.
32 devices in a mesh: dp: 16 (over z, y, x), seq: 2 (over core).
Axes of the slice: x: 2, y: 2, z: 4, core: 2. Of those that a mesh axis runs over, the one named last changes fastest.
Arguments:
- tokens: bfloat16 [16, 1024, 768], P('dp', 'seq'), may hold values from -6 to 6
- segment_ids: int32 [16, 1024], P('dp', 'seq'), may hold values from 0 to 7, never falling along the last dimension, each value on 1 to 512 neighbouring positions
- norm1_gain: bfloat16 [768], replicated, may hold values from 0.25 to 1.75
- w_query: bfloat16 [768, 768], replicated, may hold values from -0.21875 to 0.21875
- w_key: bfloat16 [768, 768], replicated, may hold values from -0.21875 to 0.21875
- w_value: bfloat16 [768, 768], replicated, may hold values from -0.21875 to 0.21875
- w_out: bfloat16 [768, 768], replicated, may hold values from -0.875 to 0.875
- norm2_gain: bfloat16 [768], replicated, may hold values from 0.25 to 1.75
- w_gate: bfloat16 [768, 2048], replicated, may hold values from -0.21875 to 0.21875
- w_up: bfloat16 [768, 2048], replicated, may hold values from -0.21875 to 0.21875
- w_down: bfloat16 [2048, 768], replicated, may hold values from -0.125 to 0.125
- out_grad: bfloat16 [16, 1024, 768], P('dp', 'seq'), may hold values from -6 to 6
Outputs:
- block_out: bfloat16 [16, 1024, 768], P('dp', 'seq')
- input_grad: bfloat16 [16, 1024, 768], P('dp', 'seq')
- norm1_gain_grad: float32 [768], P(('dp', 'seq'))
- query_grad: float32 [768, 768], P(None, ('dp', 'seq'))
- key_grad: float32 [768, 768], P(None, ('dp', 'seq'))
- value_grad: float32 [768, 768], P(None, ('dp', 'seq'))
- out_proj_grad: float32 [768, 768], P(None, ('dp', 'seq'))
- norm2_gain_grad: float32 [768], P(('dp', 'seq'))
- gate_grad: float32 [768, 2048], P(None, ('dp', 'seq'))
- up_grad: float32 [768, 2048], P(None, ('dp', 'seq'))
- down_grad: float32 [2048, 768], P(None, ('dp', 'seq'))
Inputs may be any that keep to these rules, and one draw needn't show every extreme that they name: `segment_ids`: in each sequence the ids never fall and each of the 8 ids marks one document of 1 to 512 tokens; some document has exactly 512.
All inputs are finite; a program needn't handle non-finite values.
Results may differ from a plain program's by a relative error of at most 0.013.
Values may be sent and summed in bfloat16 or wider, within the bound.
A program may use at most 192 MiB of HBM per device.

v0:
```python
import jax
import jax.numpy as jnp
from jax import lax
from jax.sharding import PartitionSpec as P

HD = 64
DOCS = 8


EPS = 1e-06
SCALE = 0.125
NEG = -1e30
BASE = 10000.0


def for_sending(array):

    def short(part):
        return part.astype(jnp.bfloat16) if part.dtype == jnp.float32 else part

    return jax.tree.map(short, array)


def rms_norm(values, gain):
    return values * lax.rsqrt(jnp.mean(values * values, axis=-1, keepdims=True) + EPS) * gain


def swiglu(gate_proj, up_proj):
    return jax.nn.silu(gate_proj) * up_proj


def rope_tables(seg_row, doc_count, head_size):
    length = seg_row.shape[0]
    onehot = (seg_row[:, None] == jnp.arange(doc_count, dtype=jnp.int32)[None, :]).astype(jnp.int32)
    counts = jnp.sum(onehot, axis=0)
    starts = jnp.cumsum(counts) - counts
    first_index = jnp.sum(onehot * starts[None, :], axis=1)
    places = (jnp.arange(length, dtype=jnp.int32) - first_index).astype(jnp.float32)
    freqs = BASE ** (-jnp.arange(head_size // 2, dtype=jnp.float32) * (2.0 / head_size))
    angles = places[:, None] * freqs[None, :]
    return (jnp.cos(angles), jnp.sin(angles))


def rotate(heads, cosine, sine_table):
    half_size = heads.shape[-1] // 2
    lower_half = heads[..., :half_size]
    upper_half = heads[..., half_size:]
    cos_wide = cosine[:, None, :]
    sin_wide = sine_table[:, None, :]
    return jnp.concatenate(
        [
            lower_half * cos_wide - upper_half * sin_wide,
            upper_half * cos_wide + lower_half * sin_wide,
        ],
        axis=-1,
    )


def prepare_row(query_part, key_part, seg_row):
    length, width = query_part.shape
    groups = width // HD
    cosine, sine_table = rope_tables(seg_row, DOCS, HD)
    q_rot = rotate(
        query_part.astype(jnp.float32).reshape(length, groups, HD), cosine, sine_table
    ).astype(jnp.bfloat16)
    k_rot = rotate(
        key_part.astype(jnp.float32).reshape(length, groups, HD), cosine, sine_table
    ).astype(jnp.bfloat16)
    return (q_rot, k_rot, cosine, sine_table)


def masked_scores(q_block, k_rot, seg_row, offset):
    row_count = q_block.shape[0]
    places = jnp.arange(seg_row.shape[0], dtype=jnp.int32)
    scores = jnp.einsum("qhd,khd->hqk", q_block, k_rot, preferred_element_type=jnp.float32) * SCALE
    allowed = (seg_row[offset : offset + row_count, None] == seg_row[None, :]) & (
        places[offset : offset + row_count, None] >= places[None, :]
    )
    return jnp.where(allowed[None], scores, NEG)


def attend_row(query_part, key_part, value_part, seg_row):
    length, width = query_part.shape
    groups = width // HD
    q_rot, k_rot, cosine, sine_table = prepare_row(query_part, key_part, seg_row)
    v_heads = value_part.reshape(length, groups, HD)
    block_rows = min(512, length)
    pieces = []
    sums = []
    for offset in range(0, length, block_rows):
        scores = masked_scores(q_rot[offset : offset + block_rows], k_rot, seg_row, offset)
        row_peak = jnp.max(scores, axis=-1, keepdims=True)
        exp_scores = jnp.exp(scores - row_peak)
        row_total = jnp.sum(exp_scores, axis=-1, keepdims=True)
        attn_probs = (exp_scores / row_total).astype(jnp.bfloat16)
        result = jnp.einsum("hqk,khd->qhd", attn_probs, v_heads, preferred_element_type=jnp.float32)
        pieces.append(result.reshape(block_rows, width).astype(jnp.bfloat16))
        sums.append((row_peak + jnp.log(row_total))[..., 0])
    return (jnp.concatenate(pieces, axis=0), jnp.concatenate(sums, axis=1))


def attend_row_back(query_part, key_part, value_part, seg_row, grad_part, log_sums):
    length, width = query_part.shape
    groups = width // HD
    q_rot, k_rot, cosine, sine_table = prepare_row(query_part, key_part, seg_row)
    v_heads = value_part.reshape(length, groups, HD)
    grad_heads = grad_part.reshape(length, groups, HD)
    block_rows = min(512, length)
    d_k_rot = jnp.zeros((length, groups, HD), jnp.float32)
    d_value = jnp.zeros((length, groups, HD), jnp.float32)
    query_parts = []
    for offset in range(0, length, block_rows):
        q_block = q_rot[offset : offset + block_rows]
        grad_block = grad_heads[offset : offset + block_rows]
        scores = masked_scores(q_block, k_rot, seg_row, offset)
        attn_probs = jnp.exp(scores - log_sums[:, offset : offset + block_rows, None])
        grad_probs = jnp.einsum(
            "qhd,khd->hqk", grad_block, v_heads, preferred_element_type=jnp.float32
        )
        row_delta = jnp.sum(attn_probs * grad_probs, axis=-1, keepdims=True)
        d_scores = (attn_probs * (grad_probs - row_delta)).astype(jnp.bfloat16)
        query_parts.append(
            jnp.einsum("hqk,khd->qhd", d_scores, k_rot, preferred_element_type=jnp.float32) * SCALE
        )
        d_k_rot = (
            d_k_rot
            + jnp.einsum("hqk,qhd->khd", d_scores, q_block, preferred_element_type=jnp.float32)
            * SCALE
        )
        d_value = d_value + jnp.einsum(
            "hqk,qhd->khd",
            attn_probs.astype(jnp.bfloat16),
            grad_block,
            preferred_element_type=jnp.float32,
        )
    d_q_rot = jnp.concatenate(query_parts, axis=0)
    d_query = rotate(d_q_rot, cosine, -sine_table).reshape(length, width).astype(jnp.bfloat16)
    d_key = rotate(d_k_rot, cosine, -sine_table).reshape(length, width).astype(jnp.bfloat16)
    return (d_query, d_key, d_value.reshape(length, width).astype(jnp.bfloat16))


def shards(
    tokens,
    segment_ids,
    norm1_gain,
    w_query,
    w_key,
    w_value,
    w_out,
    norm2_gain,
    w_gate,
    w_up,
    w_down,
    out_grad,
):
    seqs, half_len, width = tokens.shape
    row_count = seqs * half_len
    gain_first = norm1_gain.astype(jnp.float32)
    gain_second = norm2_gain.astype(jnp.float32)
    full_ids = lax.all_gather(segment_ids, "seq", axis=1, tiled=True)
    inputs = tokens.reshape(row_count, width).astype(jnp.float32)
    normed1 = rms_norm(inputs, gain_first).astype(jnp.bfloat16)
    query_proj = (
        jnp.dot(normed1, w_query, preferred_element_type=jnp.float32)
        .astype(jnp.bfloat16)
        .reshape(seqs, half_len, width)
    )
    key_proj = (
        jnp.dot(normed1, w_key, preferred_element_type=jnp.float32)
        .astype(jnp.bfloat16)
        .reshape(seqs, half_len, width)
    )
    value_proj = (
        jnp.dot(normed1, w_value, preferred_element_type=jnp.float32)
        .astype(jnp.bfloat16)
        .reshape(seqs, half_len, width)
    )
    query_heads, key_heads, value_heads = (
        lax.all_to_all(query_proj, "seq", split_axis=2, concat_axis=1, tiled=True),
        lax.all_to_all(key_proj, "seq", split_axis=2, concat_axis=1, tiled=True),
        lax.all_to_all(value_proj, "seq", split_axis=2, concat_axis=1, tiled=True),
    )
    attended_heads, log_sums = lax.map(
        lambda packed: attend_row(*packed), (query_heads, key_heads, value_heads, full_ids)
    )
    attended = jax.tree.map(
        lambda part, own: part.astype(own.dtype),
        lax.all_to_all(for_sending(attended_heads), "seq", split_axis=1, concat_axis=2, tiled=True),
        attended_heads,
    ).reshape(row_count, width)
    residual = inputs + jnp.dot(attended, w_out, preferred_element_type=jnp.float32)
    normed2 = rms_norm(residual, gain_second).astype(jnp.bfloat16)
    gate_proj = jnp.dot(normed2, w_gate, preferred_element_type=jnp.float32)
    up_proj = jnp.dot(normed2, w_up, preferred_element_type=jnp.float32)
    hidden = swiglu(gate_proj, up_proj).astype(jnp.bfloat16)
    block_out = (residual + jnp.dot(hidden, w_down, preferred_element_type=jnp.float32)).astype(
        jnp.bfloat16
    )
    upstream = out_grad.reshape(row_count, width)
    down_grad = jnp.einsum("nf,nd->fd", hidden, upstream, preferred_element_type=jnp.float32)
    d_hidden = jnp.einsum("nd,fd->nf", upstream, w_down, preferred_element_type=jnp.float32)
    unused_out, swiglu_pull = jax.vjp(swiglu, gate_proj, up_proj)
    d_gate, d_up = swiglu_pull(d_hidden)
    d_gate = d_gate.astype(jnp.bfloat16)
    d_up = d_up.astype(jnp.bfloat16)
    gate_grad = jnp.einsum("nd,nf->df", normed2, d_gate, preferred_element_type=jnp.float32)
    up_grad = jnp.einsum("nd,nf->df", normed2, d_up, preferred_element_type=jnp.float32)
    d_normed2 = jnp.einsum(
        "nf,df->nd", d_gate, w_gate, preferred_element_type=jnp.float32
    ) + jnp.einsum("nf,df->nd", d_up, w_up, preferred_element_type=jnp.float32)
    unused_norm, norm_pull = jax.vjp(rms_norm, residual, gain_second)
    d_residual, norm2_gain_grad = norm_pull(d_normed2)
    d_residual = d_residual + upstream.astype(jnp.float32)
    d_branch = d_residual.astype(jnp.bfloat16)
    out_proj_grad = jnp.einsum("nd,ne->de", attended, d_branch, preferred_element_type=jnp.float32)
    d_attended = (
        jnp.einsum("ne,de->nd", d_branch, w_out, preferred_element_type=jnp.float32)
        .astype(jnp.bfloat16)
        .reshape(seqs, half_len, width)
    )
    grad_heads = lax.all_to_all(d_attended, "seq", split_axis=2, concat_axis=1, tiled=True)
    d_query_heads, d_key_heads, d_value_heads = lax.map(
        lambda packed: attend_row_back(*packed),
        (query_heads, key_heads, value_heads, full_ids, grad_heads, log_sums),
    )
    d_query, d_key, d_value = (
        lax.all_to_all(d_query_heads, "seq", split_axis=1, concat_axis=2, tiled=True),
        lax.all_to_all(d_key_heads, "seq", split_axis=1, concat_axis=2, tiled=True),
        lax.all_to_all(d_value_heads, "seq", split_axis=1, concat_axis=2, tiled=True),
    )
    d_query = d_query.reshape(row_count, width)
    d_key = d_key.reshape(row_count, width)
    d_value = d_value.reshape(row_count, width)
    query_grad = jnp.einsum("nd,ne->de", normed1, d_query, preferred_element_type=jnp.float32)
    key_grad = jnp.einsum("nd,ne->de", normed1, d_key, preferred_element_type=jnp.float32)
    value_grad = jnp.einsum("nd,ne->de", normed1, d_value, preferred_element_type=jnp.float32)
    d_normed1 = jnp.einsum("ne,de->nd", d_query, w_query, preferred_element_type=jnp.float32)
    d_normed1 = d_normed1 + jnp.einsum(
        "ne,de->nd", d_key, w_key, preferred_element_type=jnp.float32
    )
    d_normed1 = d_normed1 + jnp.einsum(
        "ne,de->nd", d_value, w_value, preferred_element_type=jnp.float32
    )
    unused_first, first_pull = jax.vjp(rms_norm, inputs, gain_first)
    d_inputs, norm1_gain_grad = first_pull(d_normed1)
    input_grad = (d_inputs + d_residual).astype(jnp.bfloat16).reshape(seqs, half_len, width)
    terms = (
        norm1_gain_grad.reshape(1, width),
        query_grad,
        key_grad,
        value_grad,
        out_proj_grad,
        norm2_gain_grad.reshape(1, width),
        gate_grad,
        up_grad,
        down_grad,
    )
    summed = (
        lax.psum_scatter(terms[0], ("dp", "seq"), scatter_dimension=1, tiled=True),
        lax.psum_scatter(terms[1], ("dp", "seq"), scatter_dimension=1, tiled=True),
        lax.psum_scatter(terms[2], ("dp", "seq"), scatter_dimension=1, tiled=True),
        lax.psum_scatter(terms[3], ("dp", "seq"), scatter_dimension=1, tiled=True),
        lax.psum_scatter(terms[4], ("dp", "seq"), scatter_dimension=1, tiled=True),
        lax.psum_scatter(terms[5], ("dp", "seq"), scatter_dimension=1, tiled=True),
        lax.psum_scatter(terms[6], ("dp", "seq"), scatter_dimension=1, tiled=True),
        lax.psum_scatter(terms[7], ("dp", "seq"), scatter_dimension=1, tiled=True),
        lax.psum_scatter(terms[8], ("dp", "seq"), scatter_dimension=1, tiled=True),
    )
    return (
        block_out.reshape(seqs, half_len, width),
        input_grad,
        summed[0].reshape(-1),
        summed[1],
        summed[2],
        summed[3],
        summed[4],
        summed[5].reshape(-1),
        summed[6],
        summed[7],
        summed[8],
    )


def solution(mesh):
    placed = (
        P("dp", "seq", None),
        P("dp", "seq"),
        P(),
        P(),
        P(),
        P(),
        P(),
        P(),
        P(),
        P(),
        P(),
        P("dp", "seq", None),
    )
    return jax.shard_map(
        shards,
        mesh=mesh,
        in_specs=placed,
        out_specs=(
            P("dp", "seq", None),
            P("dp", "seq", None),
            P(("dp", "seq")),
            P(None, ("dp", "seq")),
            P(None, ("dp", "seq")),
            P(None, ("dp", "seq")),
            P(None, ("dp", "seq")),
            P(("dp", "seq")),
            P(None, ("dp", "seq")),
            P(None, ("dp", "seq")),
            P(None, ("dp", "seq")),
        ),
        check_vma=False,
    )
```

profile of v0, /device:TPU:0, one launch (start us, length us, event | category | flops | bytes accessed | tf_op | source)
XLA Modules:
  0.0 973.1 jit_solution(6240184245526395268)
XLA Ops:
  10.0 3.2 fusion.37
  13.2 4.8 copy.82
  18.5 7.3 reduce.2
  28.1 4.3 all-to-all-start.1
  35.7 3.2 fusion.38
  38.9 4.8 copy.84
  43.7 7.3 reduce.1
  53.3 4.5 all-to-all-start.2
  57.9 2.6 reshape.502
  60.5 3.8 copy.111
  64.2 3.4 reshape.491
  67.7 3.2 fusion.36
  70.9 4.8 copy.80
  75.7 7.3 reduce
  85.3 4.7 all-to-all-start
  92.6 3.8 copy.110
  96.4 3.4 reshape.492
  105.7 3.2 reshape.473
  116.9 2.8 fusion
  121.6 4.1 fusion.44
  127.7 3.8 fusion.77
  131.5 2.8 fusion.1
  136.2 4.0 fusion.43
  145.7 7.3 reduce.3
  155.0 4.3 all-to-all-start.3
  161.4 3.0 reshape.506
  169.2 2.8 multiply_reduce_fusion.4
  176.6 4.7 multiply_convert_fusion.2
  183.2 2.7 multiply_reduce_fusion.2
  189.9 3.4 fusion.39
  193.3 4.9 copy.90
  198.2 7.3 reduce.4
  207.9 6.4 all_to_all.108
  218.7 6.1 fusion.4
  224.9 7.0 add_convert_fusion
  231.9 4.8 copy.95
  236.7 7.3 reduce.5
  245.9 6.4 all_to_all.109
  259.6 3.8 fusion.70
  263.5 11.9 %multiply_reduce_fusion.1 = (f32[6,512]{1,0:T(8,128)}, f32[6,512,1024]{2,1,0:T(8,128)}) fusion(f32[6,512,1024]{2,1,0:T(8,128)} %copy-done.1, f32[6,512]{1,0:T(8,128)S(1)} %log_add_fusion.1, bf16[512,6,64]{0,2,1:T(8,128)(2,1)} %bitcast.222, bf16[1024,6,64]{0,2,1:T(8,128)(2,1)} %reshape.473), kind=kOutput, calls=%fused_computation.4 | convolution fusion | flops 412087296 | bytes 26370048 | tf_op jit(solution)/shard_map/while/body/eval_jaxpr/qhd,khd->hqk/dot_general | solution.py:117
  275.4 9.6 multiply_reduce_fusion
  285.1 7.5 multiply_convert_fusion.1
  292.6 4.2 fusion.42
  298.1 6.3 multiply_convert_fusion
  309.6 5.0 copy.91
  314.6 7.3 reduce.6
  323.9 6.4 all_to_all.110
  330.3 2.6 reshape.510
  337.7 3.7 fusion.66
  341.5 4.9 copy.93
  346.4 7.3 reduce.7
  355.6 6.6 all_to_all.111
  369.6 3.7 fusion.68
  373.4 6.4 fusion.85
  379.8 6.3 fusion.84
  386.2 6.2 fusion.48
  399.8 42.1 %all-reduce.2 = (f32[1,768]{1,0:T(1,128)S(1)}, f32[1,768]{1,0:T(1,128)S(1)}) all-reduce(f32[1,768]{1,0:T(1,128)S(1)} %reshape.486, f32[1,768]{1,0:T(1,128)S(1)} %reshape.488), channel_id=2, replica_groups=mesh['dp'=16,'seq'=2] {'dp','seq'}, use_global_device_ids=true, to_apply=%region_14.15.clone | all-reduce | flops 1536 | bytes 12288
  443.1 3.6 fusion.46
  446.7 2.7 fusion.40
  449.4 52.0 %reduce-scatter.10.cloned.1.call-done = f32[768,24]{0,1:T(8,128)} async-done(((f32[768,768]{0,1:T(8,128)}), f32[768,24]{0,1:T(8,128)}) %reduce-scatter.10.cloned.1.call-update) | async-done | bytes 73744 | tf_op jit(solution)/shard_map/reduce_scatter | solution.py:260
  501.4 104.3 %reduce-scatter.12.cloned.1.call-done = f32[768,24]{0,1:T(8,128)} async-done(((f32[768,768]{0,1:T(8,128)}), f32[768,24]{0,1:T(8,128)}) %reduce-scatter.12.cloned.1.call-update) | async-done | bytes 73744 | tf_op jit(solution)/shard_map/reduce_scatter | solution.py:261
  605.7 120.1 %reduce-scatter.20.cloned.1.call-done = f32[768,64]{0,1:T(8,128)} async-done(((f32[768,2048]{0,1:T(8,128)}), f32[768,64]{0,1:T(8,128)}) %reduce-scatter.20.cloned.1.call-update) | async-done | bytes 196624 | tf_op jit(solution)/shard_map/reduce_scatter | solution.py:266
  725.8 120.0 %reduce-scatter.18.cloned.1.call-done = f32[768,64]{0,1:T(8,128)} async-done(((f32[768,2048]{0,1:T(8,128)}), f32[768,64]{0,1:T(8,128)}) %reduce-scatter.18.cloned.1.call-update) | async-done | bytes 196624 | tf_op jit(solution)/shard_map/reduce_scatter | solution.py:265
  845.9 120.1 %reduce-scatter.22.cloned.1.call-done = f32[2048,24]{0,1:T(8,128)} async-done(((f32[2048,768]{0,1:T(8,128)}), f32[2048,24]{0,1:T(8,128)}) %reduce-scatter.22.cloned.1.call-update) | async-done | bytes 196624 | tf_op jit(solution)/shard_map/reduce_scatter | solution.py:267
  (228 shorter events, 107.6 us)
Async XLA Ops:
  7.2 169.4 %copy-start = (bf16[2048,768]{1,0:T(8,128)(2,1)S(1)}, bf16[2048,768]{1,0:T(8,128)(2,1)}, u32[]{:S(2)}) copy-start(bf16[2048,768]{1,0:T(8,128)(2,1)} %param.22) | copy-start | bytes 9437188
  9.3 58.4 %copy-start.39 = (f32[512]{0:T(512)}, f32[512]{0:T(512)S(1)}, u32[]{:S(2)}) copy-start(f32[512]{0:T(512)S(1)} %fusion.57) | copy-start | bytes 6148
  10.0 57.7 %copy-start.37 = (f32[768]{0:T(1024)}, f32[768]{0:T(1024)S(1)}, u32[]{:S(2)}) copy-start(f32[768]{0:T(1024)S(1)} %convert_element_type.206) | copy-start | bytes 9220
  25.8 6.7 copy-start.55
  28.1 25.2 %all-to-all-start.1 = ((bf16[2,2,98304]{2,1,0:T(2,128)(2,1)}), bf16[2,2,98304]{2,1,0:T(2,128)(2,1)}, u32[]{:S(2)}, u32[]{:S(2)}) async-start(bf16[2,2,98304]{2,1,0:T(2,128)(2,1)} %reshape.501), calls=%async_computation.1 | async-start | bytes 1572864 | tf_op jit(solution)/shard_map/all_to_all | solution.py:179
  35.7 3.2 copy-start.52
  53.3 32.0 %all-to-all-start.2 = ((bf16[2,2,98304]{2,1,0:T(2,128)(2,1)}), bf16[2,2,98304]{2,1,0:T(2,128)(2,1)}, u32[]{:S(2)}, u32[]{:S(2)}) async-start(bf16[2,2,98304]{2,1,0:T(2,128)(2,1)} %reshape.503), calls=%async_computation.2 | async-start | bytes 1572864 | tf_op jit(solution)/shard_map/all_to_all | solution.py:180
  85.3 14.5 %all-to-all-start = ((bf16[2,2,98304]{2,1,0:T(2,128)(2,1)}), bf16[2,2,98304]{2,1,0:T(2,128)(2,1)}, u32[]{:S(2)}, u32[]{:S(2)}) async-start(bf16[2,2,98304]{2,1,0:T(2,128)(2,1)} %reshape.499), calls=%async_computation | async-start | bytes 1572864 | tf_op jit(solution)/shard_map/all_to_all | solution.py:181
  110.1 2.4 copy-start.30
  110.1 2.5 slice-start.6
  110.1 2.5 copy-start.53
  112.5 4.3 copy-start.14
  112.6 4.3 copy-start.17
  112.6 4.3 copy-start.19
  112.6 15.1 %copy-start.12 = (bf16[1024,6,32]{0,2,1:T(8,128)(2,1)}, bf16[1024,6,32]{0,2,1:T(8,128)(2,1)S(1)}, u32[]{:S(2)}) copy-start(bf16[1024,6,32]{0,2,1:T(8,128)(2,1)S(1)} %get-tuple-element.83) | copy-start | bytes 1179652
  116.8 4.5 copy-start.1
  116.9 4.7 copy-start.42
  116.9 4.7 copy-start.5
  121.6 4.1 copy-start.44
  131.5 4.5 copy-start.2
  131.5 4.7 copy-start.46
  131.5 4.7 copy-start.6
  136.2 4.0 copy-start.48
  136.2 5.9 copy-start.29
  152.9 6.5 copy-start.56
  155.0 6.4 all-to-all-start.3
  159.4 290.0 %reduce-scatter.16.cloned.1.call-start = ((), (), s32[]{:S(2)}) async-start(), calls=%async_computation.18 | async-start | bytes 2433024 | tf_op jit(solution)/shard_map/reduce_scatter | solution.py:263
  169.2 3.0 copy-start.58
  172.0 14.0 %copy-start.10 = (f32[512,768]{1,0:T(8,128)}, f32[512,768]{1,0:T(8,128)S(1)}, u32[]{:S(2)}) copy-start(f32[512,768]{1,0:T(8,128)S(1)} %get-tuple-element.97) | copy-start | bytes 4718596
  172.2 1.8 copy-start.8
  172.2 2.5 copy-start.57
  174.7 1.8 copy-start.24
  181.2 1.9 copy-start.27
  181.2 2.0 copy-start.28
  189.8 259.6 %reduce-scatter.14.cloned.1.call-start = ((), (), s32[]{:S(2)}) async-start(), calls=%async_computation.17 | async-start | bytes 2433024 | tf_op jit(solution)/shard_map/reduce_scatter | solution.py:262
  216.9 1.7 copy-start.49
  218.7 6.2 copy-start.34
  218.7 6.1 copy-start.21
  263.4 238.0 %reduce-scatter.10.cloned.1.call-start = ((), (), s32[]{:S(2)}) async-start(), calls=%async_computation.15 | async-start | bytes 2433024 | tf_op jit(solution)/shard_map/reduce_scatter | solution.py:260
  263.4 12.0 %copy-start.7 = (bf16[1024,6,64]{0,2,1:T(8,128)(2,1)S(1)}, bf16[1024,6,64]{0,2,1:T(8,128)(2,1)}, u32[]{:S(2)}) copy-start(bf16[1024,6,64]{0,2,1:T(8,128)(2,1)} %reshape.473) | copy-start | bytes 2359300
  263.5 12.0 %copy-start.35 = (f32[6,512]{1,0:T(8,128)S(1)}, f32[6,512]{1,0:T(8,128)}, u32[]{:S(2)}) copy-start(f32[6,512]{1,0:T(8,128)} %copy-done.34) | copy-start | bytes 36868
  263.5 21.6 %slice-start = ((s8[12582912]{0:T(1024)(128)(4,1)}), s8[4194304]{0:T(1024)(128)(4,1)S(1)}, s32[]{:S(2)}) async-start(s8[12582912]{0:T(1024)(128)(4,1)} %bitcast.195), calls=%async_computation.22 | async-start | bytes 8388608
  263.5 21.6 %slice-start.1 = ((s8[12582912]{0:T(1024)(128)(4,1)}), s8[4194304]{0:T(1024)(128)(4,1)S(1)}, s32[]{:S(2)}) async-start(s8[12582912]{0:T(1024)(128)(4,1)} %bitcast.195), calls=%async_computation.23 | async-start | bytes 8388608
  275.4 9.6 slice-start.2
  285.1 13.0 %slice-start.3 = ((s8[12582912]{0:T(1024)(128)(4,1)}), s8[4194304]{0:T(1024)(128)(4,1)S(1)}, s32[]{:S(2)}) async-start(s8[12582912]{0:T(1024)(128)(4,1)} %bitcast.197), calls=%async_computation.25 | async-start | bytes 8388608
  285.1 13.0 %slice-start.4 = ((s8[12582912]{0:T(1024)(128)(4,1)}), s8[4194304]{0:T(1024)(128)(4,1)S(1)}, s32[]{:S(2)}) async-start(s8[12582912]{0:T(1024)(128)(4,1)} %bitcast.197), calls=%async_computation.26 | async-start | bytes 8388608
  292.6 4.2 copy-start.13
  292.6 4.2 copy-start.15
  292.6 5.5 slice-start.5
  298.1 6.4 copy-start.18
  298.1 6.4 copy-start.20
  304.5 2.0 copy-start.16
  333.0 4.8 copy-start.38
  333.0 4.8 copy-start.40
  341.4 264.3 %reduce-scatter.12.cloned.1.call-start = ((), (), s32[]{:S(2)}) async-start(), calls=%async_computation.16 | async-start | bytes 2433024 | tf_op jit(solution)/shard_map/reduce_scatter | solution.py:261
  373.3 352.5 %reduce-scatter.20.cloned.1.call-start = ((), (), s32[]{:S(2)}) async-start(), calls=%async_computation.20 | async-start | bytes 6488064 | tf_op jit(solution)/shard_map/reduce_scatter | solution.py:266
  379.8 466.1 %reduce-scatter.18.cloned.1.call-start = ((), (), s32[]{:S(2)}) async-start(), calls=%async_computation.19 | async-start | bytes 6488064 | tf_op jit(solution)/shard_map/reduce_scatter | solution.py:265
  386.2 579.8 %reduce-scatter.22.cloned.1.call-start = ((), (), s32[]{:S(2)}) async-start(), calls=%async_computation.21 | async-start | bytes 6488064 | tf_op jit(solution)/shard_map/reduce_scatter | solution.py:267
  393.1 2.5 copy-start.23
  393.1 2.5 copy-start.59
  395.6 1.7 copy-start.32
  397.3 45.7 %copy-start.51 = (f32[512]{0:T(512)S(1)}, f32[512]{0:T(512)}, u32[]{:S(2)}) copy-start(f32[512]{0:T(512)} %copy-done.50) | copy-start | bytes 6148
  443.1 3.6 copy-start.11
  443.1 3.6 copy-start.26
  (14 other events, 18.1 us)
Sparse Core Ops, SparseCore 0:
  189.9 102.3 reduce-scatter.15
  298.2 98.6 reduce-scatter.13
  402.7 98.6 reduce-scatter.9
  507.1 98.4 reduce-scatter.11
  611.7 114.0 reduce-scatter.19
  731.9 113.9 reduce-scatter.17
  852.1 113.8 reduce-scatter.21
where the time goes:
time: 981 us; the launch traced here: 973 us
  waiting for transfers between devices  519 us (53%)
  local copies, waits for them, and re-layouts  131 us (13%)
  matrix products  127 us (13%)
  other arithmetic  92.8 us (9%)
  blocking collectives  70 us (7%)
  starting transfers between devices  18.2 us (2%)
  between operations  15.3 us (2%)
    reduce_scatter x1, waiting for transfers between devices, shards(): lax.psum_scatter(terms[8], ('dp', 'seq'), scatter_dimension=1, tiled=True)  120 us
    reduce_scatter x1, waiting for transfers between devices, shards(): lax.psum_scatter(terms[7], ('dp', 'seq'), scatter_dimension=1, tiled=True)  120 us
    reduce_scatter x1, waiting for transfers between devices, shards(): lax.psum_scatter(terms[6], ('dp', 'seq'), scatter_dimension=1, tiled=True)  120 us
    reduce_scatter x1, waiting for transfers between devices, shards(): lax.psum_scatter(terms[2], ('dp', 'seq'), scatter_dimension=1, tiled=True)  104 us
    unnamed x155, local copies, waits for them, and re-layouts  60.4 us
    unnamed x10, other arithmetic  58.3 us
    reduce_scatter x1, waiting for transfers between devices, shards(): lax.psum_scatter(terms[1], ('dp', 'seq'), scatter_dimension=1, tiled=True)  52 us
    unnamed x1, blocking collectives  42.1 us
  transfers between devices with their start and end apart: 11, of which 6 were waited for; matrix products, arithmetic and copies ran while one was open for 25% of the time, Pallas kernels for 0%

commit v1 on v0

v1 whole, which is shorter than its diff:
```python
import functools

import jax
import jax.numpy as jnp
import numpy as np
from jax import lax
from jax.experimental import pallas as pl
from jax.experimental.pallas import tpu as pltpu
from jax.sharding import PartitionSpec as P

HD = 64
EPS = 1e-06
SCALE = 0.125
NEG = -1e30
BASE = 10000.0
AX = ("dp", "seq")
BF = jnp.bfloat16
F32 = jnp.float32
TB = 256
LANES = 128


def nn(a, b):
    return lax.dot_general(a, b, (((1,), (0,)), ((), ())), preferred_element_type=F32)


def nt(a, b):
    return lax.dot_general(a, b, (((1,), (1,)), ((), ())), preferred_element_type=F32)


def tn(a, b):
    return lax.dot_general(a, b, (((0,), (0,)), ((), ())), preferred_element_type=F32)


def small_tables(length):
    freqs = BASE ** (-np.arange(HD // 2, dtype=np.float64) * (2.0 / HD))
    lane_freqs = np.tile(freqs, 4)[None, :]
    fine = np.arange(64, dtype=np.float64)[:, None] * lane_freqs
    coarse = 64.0 * np.arange(length // 64, dtype=np.float64)[:, None] * lane_freqs
    return tuple(
        np.asarray(t, np.float32) for t in (np.cos(fine), np.sin(fine), np.cos(coarse), np.sin(coarse))
    )


def angle_block(tables, sub):
    cos_f, sin_f, cos_c, sin_c = tables
    ca = cos_c[pl.ds(sub, 1), :]
    sa = sin_c[pl.ds(sub, 1), :]
    cb = cos_f[...]
    sb = sin_f[...]
    low_half = (lax.broadcasted_iota(jnp.int32, (64, LANES), 1) % HD) < HD // 2
    cosine = ca * cb - sa * sb
    sine = sa * cb + ca * sb
    return cosine, jnp.where(low_half, -sine, sine), low_half


def rotate(v, cosine, sine, low_half):
    partner = jnp.where(low_half, pltpu.roll(v, LANES - HD // 2, 1), pltpu.roll(v, HD // 2, 1))
    return v * cosine + partner * sine


def window(block):
    return max(0, (block - 2) * TB)


def bias_of(seg_col, seg_row, block):
    first = window(block)
    keys = (block + 1) * TB - first
    rows = seg_col[pl.ds(block * TB, TB), :]
    cols = seg_row[:, pl.ds(first, keys)]
    q_at = block * TB + lax.broadcasted_iota(jnp.int32, (TB, keys), 0)
    k_at = first + lax.broadcasted_iota(jnp.int32, (TB, keys), 1)
    return jnp.where((rows == cols) & (k_at <= q_at), 0.0, NEG).astype(F32)


def forward_attention(
    core, own_ref, other_ref, gain_ref, wq_ref, wk_ref, wv_ref, cos_f, sin_f, cos_c, sin_c, seg_col, seg_row,
    normed_ref, q_ref, k_ref, v_ref, att_ref, lse_ref, bias_ref,
):
    s = core[0]
    half_tokens, width = own_ref.shape
    length = 2 * half_tokens
    cols = wq_ref.shape[1]
    tables = (cos_f, sin_f, cos_c, sin_c)

    def project(t, carry):
        rows = pl.ds(pl.multiple_of(t * TB, TB), TB)
        part = t // (half_tokens // TB)
        local = pl.ds(pl.multiple_of((t % (half_tokens // TB)) * TB, TB), TB)
        x = jnp.where(part == s, own_ref[local, :], other_ref[local, :]).astype(F32)
        r = lax.rsqrt(jnp.mean(x * x, axis=-1, keepdims=True) + EPS)
        normed = (x * r * gain_ref[...]).astype(BF)
        normed_ref[rows, :] = normed
        v_ref[rows, :] = nn(normed, wv_ref[...]).astype(BF)
        q = nn(normed, wq_ref[...]).astype(BF).astype(F32)
        k = nn(normed, wk_ref[...]).astype(BF).astype(F32)
        for sub in range(TB // 64):
            cosine, sine, low_half = angle_block(tables, t * (TB // 64) + sub)
            at = pl.ds(pl.multiple_of(t * TB + sub * 64, 64), 64)
            for tile in range(cols // LANES):
                lanes = slice(tile * LANES, (tile + 1) * LANES)
                part_rows = slice(sub * 64, (sub + 1) * 64)
                q_ref[at, lanes] = (rotate(q[part_rows, lanes], cosine, sine, low_half).astype(BF) * BF(SCALE)).astype(BF)
                k_ref[at, lanes] = rotate(k[part_rows, lanes], cosine, sine, low_half).astype(BF)
        return carry

    lax.fori_loop(0, length // TB, project, 0)

    for block in range(length // TB):
        first = window(block)
        keys = (block + 1) * TB - first
        bias_ref[:, :keys] = bias_of(seg_col, seg_row, block)
        rows = pl.ds(block * TB, TB)
        span = pl.ds(first, keys)

        def head(h, carry):
            lanes = pl.ds(pl.multiple_of((h // 2) * LANES, LANES), LANES)
            lane = lax.broadcasted_iota(jnp.int32, (1, LANES), 1)
            mine = (lane // HD) == (h % 2)
            q = q_ref[rows, lanes]
            qm = jnp.where(mine, q, jnp.zeros_like(q))
            scores = nt(qm, k_ref[span, lanes]) + bias_ref[:, :keys]
            peak = jnp.max(scores, axis=-1, keepdims=True)
            weights = jnp.exp(scores - peak)
            total = jnp.sum(weights, axis=-1, keepdims=True)
            probs = (weights * (1.0 / total)).astype(BF)
            result = nn(probs, v_ref[span, lanes]).astype(BF)
            att_ref[rows, lanes] = jnp.where(mine, result, att_ref[rows, lanes])
            lse_ref[rows, :] = jnp.where(lane == h, peak + jnp.log(total), lse_ref[rows, :])
            return carry

        lax.fori_loop(0, cols // HD, head, 0)


def feed_forward(
    core, slots_a, slots_b, own_ref, other_ref, att_own, att_other, gain_ref, wo_ref, wg_ref, wu_ref, wd_ref,
    dy_own, dy_other,
    res_ref, out_keep, out_send, dn_ref, pack_ref, normed, hidden, d_gate, d_up, dy_all,
):
    s = core[0]
    half_tokens, width = own_ref.shape
    length = 2 * half_tokens
    cols = att_own.shape[1]
    own_rows = pl.ds(pl.multiple_of(s * cols, cols), cols)
    other_rows = pl.ds(pl.multiple_of((1 - s) * cols, cols), cols)

    def block(t, carry):
        rows = pl.ds(pl.multiple_of(t * TB, TB), TB)
        part = t // (half_tokens // TB)
        local = pl.ds(pl.multiple_of((t % (half_tokens // TB)) * TB, TB), TB)
        is_own = part == s
        x = jnp.where(is_own, own_ref[local, :], other_ref[local, :]).astype(F32)
        dy = jnp.where(is_own, dy_own[local, :], dy_other[local, :])
        dy_all[rows, :] = dy
        residual = x + (nn(att_own[rows, :], wo_ref[own_rows, :]) + nn(att_other[rows, :], wo_ref[other_rows, :]))
        res_ref[rows, :] = residual
        r = lax.rsqrt(jnp.mean(residual * residual, axis=-1, keepdims=True) + EPS)
        n2 = (residual * r * gain_ref[...]).astype(BF)
        normed[rows, :] = n2
        gate = nn(n2, wg_ref[...])
        up = nn(n2, wu_ref[...])
        sig = 1.0 / (1.0 + jnp.exp(-gate))
        act = gate * sig
        hid = (act * up).astype(BF)
        hidden[rows, :] = hid
        down = nn(hid, wd_ref[...])

        @pl.when(is_own)
        def _():
            out_keep[local, :] = residual + down

        @pl.when(jnp.logical_not(is_own))
        def _():
            out_send[local, :] = down.astype(BF)

        d_hidden = nt(dy, wd_ref[...])
        dg = (d_hidden * up * (sig * (1.0 + gate * (1.0 - sig)))).astype(BF)
        du = (d_hidden * act).astype(BF)
        d_gate[rows, :] = dg
        d_up[rows, :] = du
        dn_ref[rows, :] = (nt(dg, wg_ref[...]) + nt(du, wu_ref[...])).astype(BF)
        return carry

    lax.fori_loop(0, length // TB, block, 0)

    wide = wg_ref.shape[1] // 8
    pieces = width // LANES

    def gate_up(o, carry):
        cut = pl.ds(pl.multiple_of(o * wide, wide), wide)
        slot = slots_b[o]
        for which, source in ((0, d_gate), (1, d_up)):
            grad = tn(source[:, cut], normed[...]).astype(BF)
            for piece in range(pieces):
                pack_ref[slot, pl.ds((which * pieces + piece) * wide, wide), :] = grad[:, piece * LANES : (piece + 1) * LANES]
        return carry

    lax.fori_loop(0, 8, gate_up, 0)
    low = width // 16
    base = 2 * pieces * wide
    deep = hidden.shape[1] // LANES
    for piece in range(deep):
        grad = tn(dy_all[...], hidden[:, piece * LANES : (piece + 1) * LANES]).astype(BF)
        for o in range(16):
            slot = slots_a[o]
            at = pl.multiple_of(base + (slot % 2) * (deep * low) + piece * low, 16)
            pack_ref[slot // 2, pl.ds(at, low), :] = grad[o * low : (o + 1) * low, :]


def backward_attention(
    core, slots_a, slots_b, own_ref, other_ref, gain_one, gain_two, wq_ref, wk_ref, wv_ref, wo_ref, dy_own, dy_other,
    res_ref, dn_own, dn_other, att_ref, normed_ref, q_ref, k_ref, v_ref, lse_ref, cos_f, sin_f, cos_c, sin_c, seg_col, seg_row,
    d_res, dn_keep, dn_send, pack_ref, d_branch, d_att, dq, dk, dv, dq_low, dk_low, dv_low, gains, bias_ref,
):
    s = core[0]
    half_tokens, width = own_ref.shape
    length = 2 * half_tokens
    cols = att_ref.shape[1]
    tables = (cos_f, sin_f, cos_c, sin_c)
    gains[...] = jnp.zeros_like(gains)

    def norm_two(t, carry):
        rows = pl.ds(pl.multiple_of(t * TB, TB), TB)
        part = t // (half_tokens // TB)
        local = pl.ds(pl.multiple_of((t % (half_tokens // TB)) * TB, TB), TB)
        is_own = part == s
        dy = jnp.where(is_own, dy_own[local, :], dy_other[local, :]).astype(F32)
        residual = res_ref[rows, :]
        dn = dn_own[rows, :].astype(F32) + dn_other[rows, :].astype(F32)
        r = lax.rsqrt(jnp.mean(residual * residual, axis=-1, keepdims=True) + EPS)
        scaled = residual * r
        e = gain_two[...] * dn
        gains[0:1, :] += jnp.sum(dn * scaled, axis=0, keepdims=True)
        grad = dy + r * (e - scaled * (r * jnp.mean(e * residual, axis=-1, keepdims=True)))
        low = grad.astype(BF)
        d_branch[rows, :] = low

        @pl.when(is_own)
        def _():
            d_res[local, :] = grad

        d_att[rows, :] = nt(low, wo_ref[...]).astype(BF)
        return carry

    lax.fori_loop(0, length // TB, norm_two, 0)

    dk[...] = jnp.zeros_like(dk)
    dv[...] = jnp.zeros_like(dv)
    for block in range(length // TB):
        first = window(block)
        keys = (block + 1) * TB - first
        bias_ref[:, :keys] = bias_of(seg_col, seg_row, block)
        rows = pl.ds(block * TB, TB)
        span = pl.ds(first, keys)

        def head(h, carry):
            lanes = pl.ds(pl.multiple_of((h // 2) * LANES, LANES), LANES)
            lane = lax.broadcasted_iota(jnp.int32, (1, LANES), 1)
            mine = (lane // HD) == (h % 2)
            q = q_ref[rows, lanes]
            qm = jnp.where(mine, q, jnp.zeros_like(q))
            do = d_att[rows, lanes]
            dom = jnp.where(mine, do, jnp.zeros_like(do))
            lse = jnp.sum(jnp.where(lane == h, lse_ref[rows, :], 0.0), axis=-1, keepdims=True)
            k = k_ref[span, lanes]
            probs = jnp.exp(nt(qm, k) + (bias_ref[:, :keys] - lse))
            d_probs = nt(dom, v_ref[span, lanes])
            delta = jnp.sum(probs * d_probs, axis=-1, keepdims=True)
            ds = (probs * (d_probs - delta)).astype(BF)
            part = nn(ds, k)
            dq[rows, lanes] = jnp.where(mine, part, dq[rows, lanes])
            dk[span, lanes] += tn(ds, qm)
            dv[span, lanes] += tn(probs.astype(BF), dom)
            return carry

        lax.fori_loop(0, cols // HD, head, 0)

    def finish(t, carry):
        rows = pl.ds(pl.multiple_of(t * TB, TB), TB)
        part = t // (half_tokens // TB)
        local = pl.ds(pl.multiple_of((t % (half_tokens // TB)) * TB, TB), TB)
        is_own = part == s
        for sub in range(TB // 64):
            cosine, sine, low_half = angle_block(tables, t * (TB // 64) + sub)
            at = pl.ds(pl.multiple_of(t * TB + sub * 64, 64), 64)
            for tile in range(cols // LANES):
                lanes = slice(tile * LANES, (tile + 1) * LANES)
                dq_low[at, lanes] = (rotate(dq[at, lanes], cosine, -sine, low_half) * SCALE).astype(BF)
                dk_low[at, lanes] = rotate(dk[at, lanes], cosine, -sine, low_half).astype(BF)
        dv_low[rows, :] = dv[rows, :].astype(BF)
        dn = nt(dq_low[rows, :], wq_ref[...]) + nt(dk_low[rows, :], wk_ref[...]) + nt(dv_low[rows, :], wv_ref[...])
        x = jnp.where(is_own, own_ref[local, :], other_ref[local, :]).astype(F32)
        r = lax.rsqrt(jnp.mean(x * x, axis=-1, keepdims=True) + EPS)
        gains[1:2, :] += jnp.sum(dn * (x * r), axis=0, keepdims=True)

        @pl.when(is_own)
        def _():
            dn_keep[local, :] = dn

        @pl.when(jnp.logical_not(is_own))
        def _():
            dn_send[local, :] = dn.astype(BF)

        return carry

    lax.fori_loop(0, length // TB, finish, 0)

    low = width // 16
    pieces = width // LANES
    for which, source in ((0, dq_low), (1, dk_low), (2, dv_low)):
        for piece in range(pieces):
            grad = tn(source[...], normed_ref[:, piece * LANES : (piece + 1) * LANES]).astype(BF)
            for o in range(8):
                at = (which * pieces + piece) * low
                pack_ref[slots_b[o], pl.ds(at, low), :] = grad[o * low : (o + 1) * low, :]
    turned = jnp.transpose(gains[...])
    turned_low = turned.astype(BF)
    rest = (turned - turned_low.astype(F32)).astype(BF)
    lane = lax.broadcasted_iota(jnp.int32, (1, LANES), 1)
    both = jnp.where(lane < LANES // 2, turned_low, pltpu.roll(rest.astype(F32), LANES // 2, 1).astype(BF))
    at_b = 3 * pieces * low
    size_a = (cols // LANES + 1) * low
    base = at_b + low
    for piece in range(cols // LANES):
        grad = tn(d_branch[...], att_ref[:, piece * LANES : (piece + 1) * LANES]).astype(BF)
        for o in range(16):
            slot = slots_a[o]
            at = pl.multiple_of(base + (slot % 2) * size_a + piece * low, 16)
            pack_ref[slot // 2, pl.ds(at, low), :] = grad[o * low : (o + 1) * low, :]
    for o in range(16):
        slot = slots_a[o]
        at = pl.multiple_of(base + (slot % 2) * size_a + (cols // LANES) * low, 16)
        pack_ref[slot // 2, pl.ds(at, low), :] = both[o * low : (o + 1) * low, :]

        @pl.when(s == o // 8)
        def _():
            pack_ref[slots_b[o % 8], pl.ds(at_b, low), :] = both[o * low : (o + 1) * low, :]


BIG = pltpu.CompilerParams(vmem_limit_bytes=60 * 1024 * 1024)


def shape(*dims, dtype=BF):
    return jax.ShapeDtypeStruct(dims, dtype)


def flat(dp, core):
    return 2 * dp + core


def swap_cores(chips):
    return [(flat(d, c), flat(d, 1 - c)) for d in range(chips) for c in range(2)]


ORDER = ((0, 1, 2, 3), (1, 0, 2, 3))


def swap_chips(step):
    return [(flat(d, c), flat(d ^ (1 << ORDER[c][step]), c)) for d in range(16) for c in range(2)]


def to_owner_half():
    return [(flat(d, c), flat(d ^ 8, c)) for d in range(16) for c in range(2) if d // 8 != c]


def slot_tables(chip, core, chips):
    if chips != 16:
        return jnp.arange(16, dtype=jnp.int32), jnp.arange(8, dtype=jnp.int32)
    owner = jnp.arange(16, dtype=jnp.int32)
    away = owner ^ chip
    x, y, z0, z1 = away & 1, (away >> 1) & 1, (away >> 2) & 1, (away >> 3) & 1
    first = jnp.where(core == 0, x, y)
    second = jnp.where(core == 0, y, x)
    slots_a = first * 8 + second * 4 + z0 * 2 + z1
    near = slots_a // 2
    return slots_a, jnp.where(core == 0, near[:8], near[8:])


def halve(pack):
    for step in range(3):
        half = pack.shape[0] // 2
        pack3 = pack.reshape(2, half, *pack.shape[1:])
        got = lax.ppermute(pack3[1], AX, swap_chips(step))
        total = pack3[0].astype(F32) + got.astype(F32)
        pack = total.astype(BF) if step < 2 else total
    return pack[0]


def last_step(total, size_b):
    kind_b = total[:size_b]
    kind_a = total[size_b:].reshape(2, -1, LANES)
    got_a = lax.ppermute(kind_a[1].astype(BF), AX, swap_chips(3))
    got_b = lax.ppermute(kind_b.astype(BF), AX, to_owner_half())
    return kind_a[0] + got_a.astype(F32), kind_b + got_b.astype(F32)


def shards(
    tokens, segment_ids, norm1_gain, w_query, w_key, w_value, w_out, norm2_gain, w_gate, w_up, w_down, out_grad,
    *, chips,
):
    seqs, half_tokens, width = tokens.shape
    length = 2 * half_tokens
    cols = w_query.shape[1] // 2
    ff = w_gate.shape[1] // 2
    core = lax.axis_index("seq")
    chip = lax.axis_index("dp")
    core_id = core.reshape(1).astype(jnp.int32)
    pairs = swap_cores(chips)
    own = tokens.reshape(half_tokens, width)
    dy_own = out_grad.reshape(half_tokens, width)
    ids = segment_ids.reshape(1, half_tokens)
    other = lax.ppermute(own, AX, pairs)
    ids_other = lax.ppermute(ids, AX, pairs)
    dy_other = lax.ppermute(dy_own, AX, pairs)
    seg_row = jnp.where(core == 0, jnp.concatenate([ids, ids_other], 1), jnp.concatenate([ids_other, ids], 1))
    seg_col = seg_row.reshape(length, 1)
    gain_one = norm1_gain.astype(F32).reshape(1, width)
    gain_two = norm2_gain.astype(F32).reshape(1, width)
    tables = tuple(jnp.asarray(t) for t in small_tables(length))
    slots_a, slots_b = slot_tables(chip, core, chips)
    half_w = pl.BlockSpec((width, cols), lambda g, c: (0, c[0]))
    half_wide = pl.BlockSpec((width, ff), lambda g, c, a, b: (0, c[0]))
    whole = lambda a: pl.BlockSpec(a.shape, lambda g, *_: (0,) * len(a.shape))

    def out_block(s):
        return pl.BlockSpec(s.shape, lambda g, *_: (0,) * len(s.shape))

    outs = (
        shape(length, width), shape(length, cols), shape(length, cols), shape(length, cols), shape(length, cols),
        shape(length, LANES, dtype=F32),
    )
    normed1, q, k, v, att, lse = pl.pallas_call(
        forward_attention,
        out_shape=outs,
        grid_spec=pltpu.PrefetchScalarGridSpec(
            num_scalar_prefetch=1,
            grid=(1,),
            in_specs=[whole(own), whole(other), whole(gain_one), half_w, half_w, half_w]
            + [whole(t) for t in tables]
            + [whole(seg_col), whole(seg_row)],
            out_specs=[out_block(o) for o in outs],
            scratch_shapes=[pltpu.VMEM((TB, 3 * TB), F32)],
        ),
        compiler_params=BIG,
        name="attention_forward",
    )(core_id, own, other, gain_one, w_query, w_key, w_value, *tables, seg_col, seg_row)
    att_other = lax.ppermute(att, AX, pairs)

    rows_one = 2 * (width // LANES) * (ff // 8) + 2 * (ff // LANES) * (width // 16)
    outs = (
        shape(length, width, dtype=F32), shape(half_tokens, width, dtype=F32), shape(half_tokens, width),
        shape(length, width), shape(8, rows_one, LANES),
    )
    residual, out_keep, out_send, dn, pack_one = pl.pallas_call(
        feed_forward,
        out_shape=outs,
        grid_spec=pltpu.PrefetchScalarGridSpec(
            num_scalar_prefetch=3,
            grid=(1,),
            in_specs=[whole(own), whole(other), whole(att), whole(att), whole(gain_two), whole(w_out), half_wide, half_wide,
                      pl.BlockSpec((ff, width), lambda g, c, a, b: (c[0], 0)), whole(own), whole(own)],
            out_specs=[out_block(o) for o in outs],
            scratch_shapes=[
                pltpu.VMEM((length, width), BF), pltpu.VMEM((length, ff), BF), pltpu.VMEM((length, ff), BF),
                pltpu.VMEM((length, ff), BF), pltpu.VMEM((length, width), BF),
            ],
        ),
        compiler_params=BIG,
        name="feed_forward",
    )(core_id, slots_a, slots_b, own, other, att, att_other, gain_two, w_out, w_gate, w_up, w_down, dy_own, dy_other)
    out_other = lax.ppermute(out_send, AX, pairs)
    block_out = (out_keep + out_other.astype(F32)).astype(BF)
    dn_other = lax.ppermute(dn, AX, pairs)

    low = width // 16
    size_b2 = 3 * (width // LANES) * low + low
    size_a2 = (cols // LANES + 1) * low
    outs = (
        shape(half_tokens, width, dtype=F32), shape(half_tokens, width, dtype=F32), shape(half_tokens, width),
        shape(8, size_b2 + 2 * size_a2, LANES),
    )
    half_w3 = pl.BlockSpec((width, cols), lambda g, c, a, b: (0, c[0]))
    inputs = (own, other, gain_one, gain_two, w_query, w_key, w_value, w_out, dy_own, dy_other, residual, dn, dn_other,
              att, normed1, q, k, v, lse, *tables, seg_col, seg_row)
    specs = [whole(a) for a in inputs]
    specs[4] = specs[5] = specs[6] = half_w3
    specs[7] = pl.BlockSpec((cols, width), lambda g, c, a, b: (c[0], 0))
    d_res, dn_keep, dn_send, pack_two = pl.pallas_call(
        backward_attention,
        out_shape=outs,
        grid_spec=pltpu.PrefetchScalarGridSpec(
            num_scalar_prefetch=3,
            grid=(1,),
            in_specs=specs,
            out_specs=[out_block(o) for o in outs],
            scratch_shapes=[
                pltpu.VMEM((length, width), BF), pltpu.VMEM((length, cols), BF),
                pltpu.VMEM((length, cols), F32), pltpu.VMEM((length, cols), F32), pltpu.VMEM((length, cols), F32),
                pltpu.VMEM((length, cols), BF), pltpu.VMEM((length, cols), BF), pltpu.VMEM((length, cols), BF),
                pltpu.VMEM((LANES, width), F32), pltpu.VMEM((TB, 3 * TB), F32),
            ],
        ),
        compiler_params=BIG,
        name="attention_backward",
    )(core_id, slots_a, slots_b, *inputs)
    dn1 = dn_keep + lax.ppermute(dn_send, AX, pairs).astype(F32)
    x = own.astype(F32)
    r = lax.rsqrt(jnp.mean(x * x, axis=-1, keepdims=True) + EPS)
    e = gain_one * dn1
    input_grad = (d_res + r * e - x * (r * r * r) * jnp.mean(e * x, axis=-1, keepdims=True)).astype(BF)

    pieces = width // LANES
    wide = ff // 8
    size_b1 = 2 * pieces * wide
    size_a1 = (ff // LANES) * low

    if chips == 16:
        one_a, one_b = last_step(halve(pack_one), size_b1)
        two_a, two_b = last_step(halve(pack_two), size_b2)
        holds = (chip >> 3) == core

        def share(a):
            parts = a.reshape(a.shape[0], 2, a.shape[1] // 2, LANES)
            mine = jnp.where(core == 0, parts[:, 0], parts[:, 1])
            theirs = jnp.where(core == 0, parts[:, 1], parts[:, 0])
            return mine, lax.ppermute(theirs, AX, pairs)

        def both(a):
            mine, got = share(a)
            return jnp.where(core == 0, mine, got), jnp.where(core == 0, got, mine)

        def one(a):
            mine, got = share(a)
            return jnp.where(holds, mine, got)

        down_lo, down_hi = both(one_a.reshape(ff // LANES, low, LANES))
        kind_a = two_a.reshape(cols // LANES + 1, low, LANES)
        out_lo, out_hi = both(kind_a)
        gates = one(one_b.reshape(2 * pieces, wide, LANES))
        rest = one(two_b.reshape(3 * pieces + 1, low, LANES))

        def turn(a):
            return jnp.transpose(a, (0, 2, 1)).reshape(-1, a.shape[1])

        tiles = cols // LANES
        gain1 = out_lo[tiles] + out_hi[tiles]
        gain1 = gain1[:, 1] + gain1[:, 1 + LANES // 2]
        gain2 = rest[3 * pieces]
        gain2 = gain2[:, 0] + gain2[:, LANES // 2]
        summed = (
            gain1,
            turn(rest[:pieces]),
            turn(rest[pieces : 2 * pieces]),
            turn(rest[2 * pieces : 3 * pieces]),
            turn(jnp.concatenate([out_lo[:tiles], out_hi[:tiles]])),
            gain2,
            turn(gates[:pieces]),
            turn(gates[pieces:]),
            turn(jnp.concatenate([down_lo, down_hi])),
        )
    else:
        def plain_b(rows, count, size, at):
            part = rows[:, at : at + count * size].reshape(8, count, size, LANES)
            part = jnp.transpose(part, (1, 3, 0, 2)).reshape(count * LANES, 8 * size).astype(F32)
            zero = jnp.zeros_like(part)
            return jnp.where(core == 0, jnp.concatenate([part, zero], 1), jnp.concatenate([zero, part], 1))

        def plain_a(rows, count, at, each):
            part = rows[:, at:].reshape(8, 2, each, low, LANES)[:, :, :count].reshape(16, count, low, LANES)
            part = jnp.transpose(part, (1, 3, 0, 2)).reshape(count * LANES, 16 * low).astype(F32)
            zero = jnp.zeros_like(part)
            return jnp.where(core == 0, jnp.concatenate([part, zero], 0), jnp.concatenate([zero, part], 0))

        def scatter(a):
            return lax.psum_scatter(a, AX, scatter_dimension=1, tiled=True)

        tiles = cols // LANES
        gain_a = pack_two[:, size_b2:].reshape(16, tiles + 1, low, LANES)[:, tiles].astype(F32)
        gain_a = gain_a[:, :, : LANES // 2] + gain_a[:, :, LANES // 2 :]
        gain_a = gain_a.reshape(width, LANES // 2)
        gain1 = gain_a[:, 1].reshape(1, width)
        gain2 = jnp.where(core == 0, gain_a[:, 0], 0.0).reshape(1, width)
        n = pieces * low
        summed = (
            scatter(gain1).reshape(-1),
            scatter(plain_b(pack_two, pieces, low, 0)),
            scatter(plain_b(pack_two, pieces, low, n)),
            scatter(plain_b(pack_two, pieces, low, 2 * n)),
            scatter(plain_a(pack_two, tiles, size_b2, tiles + 1)),
            scatter(gain2).reshape(-1),
            scatter(plain_b(pack_one, pieces, wide, 0)),
            scatter(plain_b(pack_one, pieces, wide, pieces * wide)),
            scatter(plain_a(pack_one, ff // LANES, size_b1, ff // LANES)),
        )
    return (block_out.reshape(seqs, half_tokens, width), input_grad.reshape(seqs, half_tokens, width), *summed)


def solution(mesh):
    placed = (P("dp", "seq", None), P("dp", "seq"), *([P()] * 9), P("dp", "seq", None))
    column = P(None, AX)
    return jax.shard_map(
        functools.partial(shards, chips=mesh.shape["dp"]),
        mesh=mesh,
        in_specs=placed,
        out_specs=(
            P("dp", "seq", None), P("dp", "seq", None), P(AX), column, column, column, column, P(AX), column, column, column,
        ),
        check_vma=False,
    )
```

time: 981 us -> 219 us (0.22)
  waiting for transfers between devices: 519 us -> 64.2 us
  matrix products: 127 us -> 0 us
  local copies, waits for them, and re-layouts: 131 us -> 14.4 us
  Pallas kernels: 0 us -> 103 us
  other arithmetic: 92.8 us -> 16.9 us
  blocking collectives: 70 us -> 0 us
  between operations: 15.3 us -> 1 us
    reduce_scatter x7 -> x0, waiting for transfers between devices: 517 us -> none  [the longest x1 120 us: shards(): lax.psum_scatter(terms[8], ('dp', 'seq'), scatter_dimension=1, tiled=True)]
    dot_general x33 -> x0, matrix products: 127 us -> none  [the longest x2 21.5 us: attend_row_back(): jnp.einsum('qhd,khd->hqk', grad_block, v_heads, preferred_element_type=jn...]
    pallas_call x0 -> x3, Pallas kernels: none -> 103 us  [the longest x1 44.3 us: shards(): pl.pallas_call(backward_attention, out_shape=outs, grid_spec=pltpu.Prefet...]
    ppermute x0 -> x21, waiting for transfers between devices: none -> 64.2 us  [the longest x6 37.1 us: halve(): got = lax.ppermute(pack3[1], AX, swap_chips(step))]
    unnamed x10 -> x0, other arithmetic: 58.3 us -> none
    unnamed x155 -> x26, local copies, waits for them, and re-layouts: 60.4 us -> 3.65 us
    unnamed x1 -> x0, blocking collectives: 42.1 us -> none
    convert_element_type x9 -> x4, local copies, waits for them, and re-layouts: 33 us -> 0.09 us  [the longest x2 0.07 us: last_step(): got_b = lax.ppermute(kind_b.astype(BF), AX, to_owner_half())]
  transfers between devices with their start and end apart: 11 -> 21, of which waited for: 6 -> 11; matrix products, arithmetic and copies ran while one was open for 25% -> 10% of each run, Pallas kernels for 0% -> 31%
where the time goes in v1:
time: 219 us
  Pallas kernels  103 us (47%)
  waiting for transfers between devices  64.2 us (29%)
  starting transfers between devices  19.3 us (9%)
  other arithmetic  16.9 us (8%)
  local copies, waits for them, and re-layouts  14.4 us (7%)
    pallas_call x1, Pallas kernels, shards(): pl.pallas_call(backward_attention, out_shape=outs, grid_spec=pltpu.Prefet...  44.3 us
    ppermute x6, waiting for transfers between devices, halve(): got = lax.ppermute(pack3[1], AX, swap_chips(step))  37.1 us
    pallas_call x1, Pallas kernels, shards(): pl.pallas_call(feed_forward, out_shape=outs, grid_spec=pltpu.PrefetchScal...  34.7 us
    pallas_call x1, Pallas kernels, shards(): pl.pallas_call(forward_attention, out_shape=outs, grid_spec=pltpu.Prefetc...  24.3 us
    ppermute x2, waiting for transfers between devices, last_step(): got_b = lax.ppermute(kind_b.astype(BF), AX, to_owner_half())  18.9 us
    ppermute x6, starting transfers between devices, halve(): got = lax.ppermute(pack3[1], AX, swap_chips(step))  10 us
    slice x6, local copies, waits for them, and re-layouts, halve(): got = lax.ppermute(pack3[1], AX, swap_chips(step))  6.09 us
    convert_element_type x4, other arithmetic, halve(): pack = total.astype(BF) if step < 2 else total  4.69 us
  transfers between devices with their start and end apart: 21, of which 11 were waited for; matrix products, arithmetic and copies ran while one was open for 10% of the time, Pallas kernels for 31%

profile of v1, /device:TPU:0, one launch (start us, length us, event | category | flops | bytes accessed | tf_op | source)
XLA Modules:
  0.0 218.9 jit_solution(6984265219170209616)
XLA Ops:
  0.6 0.6 collective-permute-start
  1.2 0.1 collective-permute-start.1
  1.3 0.4 collective-permute-start.3
  1.7 1.3 reshape.270.gain_ref.gain_one
  3.0 0.4 collective-permute-done.1
  3.3 0.8 pad_add_fusion.1
  4.1 0.2 copy.98
  4.3 0.2 copy.99
  4.6 1.4 broadcast_select_fusion.3.seg_row
  5.9 0.9 broadcast_select_fusion.seg_col
  6.8 0.9 copy-done.1
  7.7 24.3 %attention_forward.1 = (bf16[1024,768]{1,0:T(8,128)(2,1)}, bf16[1024,384]{1,0:T(8,128)(2,1)}, bf16[1024,384]{1,0:T(8,128)(2,1)}, bf16[1024,384]{1,0:T(8,128)(2,1...) custom-call(s32[1]{0:T(128)} %bitcast.core, bf16[512,768]{1,0:T(8,128)(2,1)} %bitcast.140, bf16[512,768]{1,0:T(8,128)(2,1)} %copy-done.1, ...), custom_call_target="tpu_custom_call" | custom-call | tf_op jit(solution)/shard_map/attention_forward/pallas_call | solution.py:432
  31.9 0.4 collective-permute-start.2
  32.3 0.6 reshape.284.gain_ref.gain_two
  32.9 0.5 and_select_fusion
  33.4 0.6 broadcast_select_fusion.4.slots_b
  34.0 0.4 collective-permute-done.2.att_other
  34.4 0.4 copy-done.3
  34.8 0.4 copy-done.8
  35.3 34.7 %feed_forward.1 = (f32[1024,768]{1,0:T(8,128)}, f32[512,768]{1,0:T(8,128)}, bf16[512,768]{1,0:T(8,128)(2,1)}, bf16[1024,768]{1,0:T(8,128)(2,1)}, bf16[8,2304,128]{2,1,0:T(8,128)(2,1)}) custom-call(s32[1]{0:T(128)} %bitcast.core, s32[16]{0:T(128)} %get-tuple-element.44.slots_a, s32[8]{0:T(128)} %broadcast_select_fusion.4.slots_b, bf16[512,768]{1,0:T(8,128)(2,1)} %bitcast.141, ...), custom_call_target="tpu_custom_call" | custom-call | tf_op jit(solution)/shard_map/feed_forward/pallas_call | solution.py:454
  70.0 3.4 %slice.195 = bf16[4,2304,128]{2,1,0:T(8,128)(2,1)} slice(bf16[8,2304,128]{2,1,0:T(8,128)(2,1)} %get-tuple-element.40), slice={[4:8], [0:2304], [0:128]} | slice | bytes 4718592 | tf_op jit(solution)/shard_map/slice | solution.py:383
  73.4 2.8 %collective-permute-start.14 = (bf16[4,2304,128]{2,1,0:T(8,128)(2,1)}, bf16[4,2304,128]{2,1,0:T(8,128)(2,1)S(1)}, u32[]{:S(2)}, u32[]{:S(2)}) collective-permute-start(bf16[4,2304,128]{2,1,0:T(8,128)(2,1)} %slice.195), channel_id=1, source_target_pairs={{0,2},{1,5},{2,0},{3,7},{4,6},{5,1},{6,4},{7,3},{8,10},{9,13},{10,... | collective-permute-start | bytes 7077896 | tf_op jit(solution)/shard_map/ppermute | solution.py:383
  76.3 0.5 collective-permute-start.4
  76.8 2.9 %collective-permute-done.5.dn_other = bf16[1024,768]{1,0:T(8,128)(2,1)S(1)} collective-permute-done((bf16[1024,768]{1,0:T(8,128)(2,1)S(1)}, bf16[1024,768]{1,0:T(8,128)(2,1)S(1)}, u32[]{:S(2)}, u32[]{:S(2)}) %collective-permute-start.5) | collective-permute-done | bytes 1572896 | tf_op jit(solution)/shard_map/ppermute | solution.py:473
  79.7 1.2 copy-done.6
  80.9 44.3 %attention_backward.1 = (f32[512,768]{1,0:T(8,128)}, f32[512,768]{1,0:T(8,128)}, bf16[512,768]{1,0:T(8,128)(2,1)}, bf16[8,1296,128]{2,1,0:T(8,128)(2,1)}) custom-call(s32[1]{0:T(128)} %bitcast.core, s32[16]{0:T(128)} %get-tuple-element.44.slots_a, s32[8]{0:T(128)} %broadcast_select_fusion.4.slots_b, bf16[512,768]{1,0:T(8,128)(2,1)} %bitcast.142, ...), custom_call_target="tpu_custom_call" | custom-call | tf_op jit(solution)/shard_map/attention_backward/pallas_call | solution.py:488
  125.2 2.5 %slice.169 = bf16[4,1296,128]{2,1,0:T(8,128)(2,1)} slice(bf16[8,1296,128]{2,1,0:T(8,128)(2,1)} %get-tuple-element.39), slice={[4:8], [0:1296], [0:128]} | slice | bytes 2654208 | tf_op jit(solution)/shard_map/slice | solution.py:383
  127.6 1.0 collective-permute-start.7
  128.7 2.5 %fusion.5 = bf16[1,512,768]{2,1,0:T(8,128)(2,1)} fusion(f32[512,768]{1,0:T(8,128)} %get-tuple-element.27, bf16[512,768]{1,0:T(8,128)(2,1)S(1)} %collective-permute-done.4), kind=kLoop, calls=%fused_computation.15 | loop fusion | flops 1179648 | bytes 3145728 | tf_op jit(solution)/shard_map/reshape | solution.py:595
  131.2 0.3 collective-permute-start.6
  131.5 2.4 %add_convert_fusion = bf16[4,2304,128]{2,1,0:T(8,128)(2,1)S(1)} fusion(bf16[4,2304,128]{2,1,0:T(8,128)(2,1)S(1)} %collective-permute-done.14, bf16[8,2304,128]{2,1,0:T(8,128)(2,1)} %get-tuple-element.40), kind=kLoop, calls=%fused_computation | loop fusion | flops 4718592 | bytes 7077888 | tf_op jit(solution)/shard_map/convert_element_type | solution.py:385
  133.9 0.1 slice.234
  134.0 0.8 collective-permute-start.15
  134.8 19.7 %collective-permute-done.7 = bf16[4,1296,128]{2,1,0:T(8,128)(2,1)} collective-permute-done((bf16[4,1296,128]{2,1,0:T(8,128)(2,1)}, bf16[4,1296,128]{2,1,0:T(8,128)(2,1)}, u32[]{:S(2)}, u32[]{:S(2)}) %collective-permute-start.7) | collective-permute-done | bytes 1327136 | tf_op jit(solution)/shard_map/ppermute | solution.py:383
  154.5 1.8 add_convert_fusion.1
  156.3 2.0 collective-permute-start.8
  158.4 0.5 fusion
  159.0 8.1 %collective-permute-done.8 = bf16[2,1296,128]{2,1,0:T(8,128)(2,1)S(1)} collective-permute-done((bf16[2,1296,128]{2,1,0:T(8,128)(2,1)S(1)}, bf16[2,1296,128]{2,1,0:T(8,128)(2,1)S(1)}, u32[]{:S(2)}, u32[]{:S(2)}) %collective-permute-start.8) | collective-permute-done | bytes 663584 | tf_op jit(solution)/shard_map/ppermute | solution.py:383
  167.1 0.2 add_convert_fusion.4
  167.3 1.7 collective-permute-start.9
  168.9 1.4 fusion.6
  170.4 5.1 %collective-permute-done.9 = bf16[1,1296,128]{2,1,0:T(8,128)(2,1)S(1)} collective-permute-done((bf16[1,1296,128]{2,1,0:T(8,128)(2,1)S(1)}, bf16[1,1296,128]{2,1,0:T(8,128)(2,1)S(1)}, u32[]{:S(2)}, u32[]{:S(2)}) %collective-permute-start.9) | collective-permute-done | bytes 331808 | tf_op jit(solution)/shard_map/ppermute | solution.py:383
  175.6 2.7 %collective-permute-start.10 = (bf16[192,128]{1,0:T(8,128)(2,1)S(1)}, bf16[192,128]{1,0:T(8,128)(2,1)S(1)}, u32[]{:S(2)}, u32[]{:S(2)}) collective-permute-start(bf16[192,128]{1,0:T(8,128)(2,1)S(1)} %fusion.16), channel_id=1, source_target_pairs={{0,16},{1,17},{2,18},{3,19},{4,20},{5,21},{6,22},{7,23},{8,24},{9,... | collective-permute-start | bytes 147464 | tf_op jit(solution)/shard_map/ppermute | solution.py:392
  178.2 0.3 add_convert_fusion.2
  178.6 1.6 collective-permute-start.16
  180.2 0.5 collective-permute-done.10
  180.8 0.1 collective-permute-start.11
  180.9 1.3 collective-permute-start.12
  182.3 0.6 copy.163
  182.9 0.7 fusion.18
  183.6 6.2 %collective-permute-done.12 = bf16[912,128]{1,0:T(8,128)(2,1)S(1)} collective-permute-done((bf16[912,128]{1,0:T(8,128)(2,1)S(1)}, bf16[912,128]{1,0:T(8,128)(2,1)S(1)}, u32[]{:S(2)}, u32[]{:S(2)}) %collective-permute-start.12) | collective-permute-done | bytes 233504 | tf_op jit(solution)/shard_map/ppermute | solution.py:393
  189.9 4.3 %collective-permute-done.16 = bf16[1,2304,128]{2,1,0:T(8,128)(2,1)S(1)} collective-permute-done((bf16[1,2304,128]{2,1,0:T(8,128)(2,1)S(1)}, bf16[1,2304,128]{2,1,0:T(8,128)(2,1)S(1)}, u32[]{:S(2)}, u32[]{:S(2)}) %collective-permute-start.16) | collective-permute-done | bytes 589856 | tf_op jit(solution)/shard_map/ppermute | solution.py:383
  194.2 0.2 convert_add_fusion
  194.5 1.5 collective-permute-start.13
  195.9 4.0 %collective-permute-done.19 = bf16[384,128]{1,0:T(8,128)(2,1)S(1)} collective-permute-done((bf16[384,128]{1,0:T(8,128)(2,1)S(1)}, bf16[384,128]{1,0:T(8,128)(2,1)S(1)}, u32[]{:S(2)}, u32[]{:S(2)}) %collective-permute-start.19) | collective-permute-done | bytes 98336 | tf_op jit(solution)/shard_map/ppermute | solution.py:392
  200.1 1.3 collective-permute-start.17
  201.5 0.7 copy_bitcast_fusion.2
  202.2 12.7 %collective-permute-done.17 = bf16[1536,128]{1,0:T(8,128)(2,1)S(1)} collective-permute-done((bf16[1536,128]{1,0:T(8,128)(2,1)S(1)}, bf16[1536,128]{1,0:T(8,128)(2,1)S(1)}, u32[]{:S(2)}, u32[]{:S(2)}) %collective-permute-start.17) | collective-permute-done | bytes 393248 | tf_op jit(solution)/shard_map/ppermute | solution.py:393
  215.1 0.4 fusion.10
  215.6 0.6 copy.164
  216.2 0.7 fusion.17
  216.9 0.7 copy_bitcast_fusion.4
  217.6 0.5 fusion.9
  218.1 0.8 copy_bitcast_fusion
  (62 shorter events, 1.1 us)
Async XLA Ops:
  0.6 6.1 %collective-permute-start = (bf16[512,768]{1,0:T(8,128)(2,1)}, bf16[512,768]{1,0:T(8,128)(2,1)S(1)}, u32[]{:S(2)}, u32[]{:S(2)}) collective-permute-start(bf16[512,768]{1,0:T(8,128)(2,1)} %bitcast.139), channel_id=1, source_target_pairs={{0,1},{1,0},{2,3},{3,2},{4,5},{5,4},{6,7},{7,6},{8,9},{9,8},{10,11... | collective-permute-start | bytes 2359304 | tf_op jit(solution)/shard_map/ppermute | solution.py:412
  1.2 2.1 collective-permute-start.1
  1.3 32.7 %collective-permute-start.3 = (bf16[512,768]{1,0:T(8,128)(2,1)}, bf16[512,768]{1,0:T(8,128)(2,1)S(1)}, u32[]{:S(2)}, u32[]{:S(2)}) collective-permute-start(bf16[512,768]{1,0:T(8,128)(2,1)} %bitcast.145), channel_id=1, source_target_pairs={{0,1},{1,0},{2,3},{3,2},{4,5},{5,4},{6,7},{7,6},{8,9},{9,8},{10,11... | collective-permute-start | bytes 2359304 | tf_op jit(solution)/shard_map/ppermute | solution.py:414
  6.8 0.9 copy-start.1
  7.7 24.6 %copy-start.10 = (bf16[768]{0:T(1024)(128)(2,1)S(1)}, bf16[768]{0:T(1024)(128)(2,1)}, u32[]{:S(2)}) copy-start(bf16[768]{0:T(1024)(128)(2,1)} %param.23) | copy-start | bytes 4612
  31.9 2.5 %collective-permute-start.2 = (bf16[1024,384]{1,0:T(8,128)(2,1)}, bf16[1024,384]{1,0:T(8,128)(2,1)S(1)}, u32[]{:S(2)}, u32[]{:S(2)}) collective-permute-start(bf16[1024,384]{1,0:T(8,128)(2,1)} %get-tuple-element.26.att_own.att_ref), channel_id=1, source_target_pairs={{0,1},{1,0},{2,3},{3,2},{4,5},{5,4},{6,7},{7,6},{8,9},{9,8},{10,11... | collective-permute-start | bytes 2359304 | tf_op jit(solution)/shard_map/ppermute | solution.py:447
  34.0 0.9 copy-start.3
  34.4 0.9 copy-start.8
  70.0 6.3 %copy-start.5 = (bf16[1024,768]{1,0:T(8,128)(2,1)S(1)}, bf16[1024,768]{1,0:T(8,128)(2,1)}, u32[]{:S(2)}) copy-start(bf16[1024,768]{1,0:T(8,128)(2,1)} %get-tuple-element.30.dn_own) | copy-start | bytes 4718596
  73.4 58.1 %collective-permute-start.14 = (bf16[4,2304,128]{2,1,0:T(8,128)(2,1)}, bf16[4,2304,128]{2,1,0:T(8,128)(2,1)S(1)}, u32[]{:S(2)}, u32[]{:S(2)}) collective-permute-start(bf16[4,2304,128]{2,1,0:T(8,128)(2,1)} %slice.195), channel_id=1, source_target_pairs={{0,2},{1,5},{2,0},{3,7},{4,6},{5,1},{6,4},{7,3},{8,10},{9,13},{10,... | collective-permute-start | bytes 7077896 | tf_op jit(solution)/shard_map/ppermute | solution.py:383
  76.3 3.4 %collective-permute-start.5 = (bf16[1024,768]{1,0:T(8,128)(2,1)S(1)}, bf16[1024,768]{1,0:T(8,128)(2,1)S(1)}, u32[]{:S(2)}, u32[]{:S(2)}) collective-permute-start(bf16[1024,768]{1,0:T(8,128)(2,1)S(1)} %copy-done.5), channel_id=1, source_target_pairs={{0,1},{1,0},{2,3},{3,2},{4,5},{5,4},{6,7},{7,6},{8,9},{9,8},{10,11... | collective-permute-start | bytes 4718600 | tf_op jit(solution)/shard_map/ppermute | solution.py:473
  76.3 52.4 %collective-permute-start.4 = (bf16[512,768]{1,0:T(8,128)(2,1)}, bf16[512,768]{1,0:T(8,128)(2,1)S(1)}, u32[]{:S(2)}, u32[]{:S(2)}) collective-permute-start(bf16[512,768]{1,0:T(8,128)(2,1)} %get-tuple-element.28), channel_id=1, source_target_pairs={{0,1},{1,0},{2,3},{3,2},{4,5},{5,4},{6,7},{7,6},{8,9},{9,8},{10,11... | collective-permute-start | bytes 2359304 | tf_op jit(solution)/shard_map/ppermute | solution.py:471
  79.7 1.2 copy-start.6
  125.1 3.5 %copy-start.9 = (bf16[768]{0:T(1024)(128)(2,1)S(1)}, bf16[768]{0:T(1024)(128)(2,1)}, u32[]{:S(2)}) copy-start(bf16[768]{0:T(1024)(128)(2,1)} %param.18) | copy-start | bytes 4612
  127.6 26.9 %collective-permute-start.7 = (bf16[4,1296,128]{2,1,0:T(8,128)(2,1)}, bf16[4,1296,128]{2,1,0:T(8,128)(2,1)}, u32[]{:S(2)}, u32[]{:S(2)}) collective-permute-start(bf16[4,1296,128]{2,1,0:T(8,128)(2,1)} %slice.169), channel_id=1, source_target_pairs={{0,2},{1,5},{2,0},{3,7},{4,6},{5,1},{6,4},{7,3},{8,10},{9,13},{10,... | collective-permute-start | bytes 3981320 | tf_op jit(solution)/shard_map/ppermute | solution.py:383
  128.6 2.5 %copy-start.11 = (bf16[512,768]{1,0:T(8,128)(2,1)S(1)}, bf16[512,768]{1,0:T(8,128)(2,1)}, u32[]{:S(2)}) copy-start(bf16[512,768]{1,0:T(8,128)(2,1)} %get-tuple-element.38) | copy-start | bytes 2359300
  131.2 27.2 %collective-permute-start.6 = (bf16[512,768]{1,0:T(8,128)(2,1)S(1)}, bf16[512,768]{1,0:T(8,128)(2,1)S(1)}, u32[]{:S(2)}, u32[]{:S(2)}) collective-permute-start(bf16[512,768]{1,0:T(8,128)(2,1)S(1)} %copy-done.11), channel_id=1, source_target_pairs={{0,1},{1,0},{2,3},{3,2},{4,5},{5,4},{6,7},{7,6},{8,9},{9,8},{10,11... | collective-permute-start | bytes 2359304 | tf_op jit(solution)/shard_map/ppermute | solution.py:506
  131.5 23.0 %copy-start.4 = (bf16[8,1296,128]{2,1,0:T(8,128)(2,1)S(1)}, bf16[8,1296,128]{2,1,0:T(8,128)(2,1)}, u32[]{:S(2)}) copy-start(bf16[8,1296,128]{2,1,0:T(8,128)(2,1)} %get-tuple-element.39) | copy-start | bytes 7962628
  134.0 44.2 %collective-permute-start.15 = (bf16[2,2304,128]{2,1,0:T(8,128)(2,1)S(1)}, bf16[2,2304,128]{2,1,0:T(8,128)(2,1)S(1)}, u32[]{:S(2)}, u32[]{:S(2)}) collective-permute-start(bf16[2,2304,128]{2,1,0:T(8,128)(2,1)S(1)} %slice.234), channel_id=1, source_target_pairs={{0,4},{1,3},{2,6},{3,1},{4,0},{5,7},{6,2},{7,5},{8,12},{9,11},{10,... | collective-permute-start | bytes 3538952 | tf_op jit(solution)/shard_map/ppermute | solution.py:383
  154.5 3.9 %copy-start.2 = (f32[512,768]{1,0:T(8,128)S(1)}, f32[512,768]{1,0:T(8,128)}, u32[]{:S(2)}) copy-start(f32[512,768]{1,0:T(8,128)} %get-tuple-element.37) | copy-start | bytes 4718596
  156.3 2.1 copy-start
  156.3 10.7 %collective-permute-start.8 = (bf16[2,1296,128]{2,1,0:T(8,128)(2,1)S(1)}, bf16[2,1296,128]{2,1,0:T(8,128)(2,1)S(1)}, u32[]{:S(2)}, u32[]{:S(2)}) collective-permute-start(bf16[2,1296,128]{2,1,0:T(8,128)(2,1)S(1)} %slice.211), channel_id=1, source_target_pairs={{0,4},{1,3},{2,6},{3,1},{4,0},{5,7},{6,2},{7,5},{8,12},{9,11},{10,... | collective-permute-start | bytes 1990664 | tf_op jit(solution)/shard_map/ppermute | solution.py:383
  158.9 10.0 %copy-start.7 = (f32[512,768]{1,0:T(8,128)S(1)}, f32[512,768]{1,0:T(8,128)}, u32[]{:S(2)}) copy-start(f32[512,768]{1,0:T(8,128)} %get-tuple-element.36) | copy-start | bytes 4718596
  167.3 8.2 %collective-permute-start.9 = (bf16[1,1296,128]{2,1,0:T(8,128)(2,1)S(1)}, bf16[1,1296,128]{2,1,0:T(8,128)(2,1)S(1)}, u32[]{:S(2)}, u32[]{:S(2)}) collective-permute-start(bf16[1,1296,128]{2,1,0:T(8,128)(2,1)S(1)} %slice.213), channel_id=1, source_target_pairs={{0,8},{1,9},{2,10},{3,11},{4,12},{5,13},{6,14},{7,15},{8,0},{9,1},... | collective-permute-start | bytes 995336 | tf_op jit(solution)/shard_map/ppermute | solution.py:383
  175.6 5.2 %collective-permute-start.10 = (bf16[192,128]{1,0:T(8,128)(2,1)S(1)}, bf16[192,128]{1,0:T(8,128)(2,1)S(1)}, u32[]{:S(2)}, u32[]{:S(2)}) collective-permute-start(bf16[192,128]{1,0:T(8,128)(2,1)S(1)} %fusion.16), channel_id=1, source_target_pairs={{0,16},{1,17},{2,18},{3,19},{4,20},{5,21},{6,22},{7,23},{8,24},{9,... | collective-permute-start | bytes 147464 | tf_op jit(solution)/shard_map/ppermute | solution.py:392
  178.6 15.6 %collective-permute-start.16 = (bf16[1,2304,128]{2,1,0:T(8,128)(2,1)S(1)}, bf16[1,2304,128]{2,1,0:T(8,128)(2,1)S(1)}, u32[]{:S(2)}, u32[]{:S(2)}) collective-permute-start(bf16[1,2304,128]{2,1,0:T(8,128)(2,1)S(1)} %slice.236), channel_id=1, source_target_pairs={{0,8},{1,9},{2,10},{3,11},{4,12},{5,13},{6,14},{7,15},{8,0},{9,1},... | collective-permute-start | bytes 1769480 | tf_op jit(solution)/shard_map/ppermute | solution.py:383
  180.8 1.4 collective-permute-start.11
  180.9 9.0 %collective-permute-start.12 = (bf16[912,128]{1,0:T(8,128)(2,1)S(1)}, bf16[912,128]{1,0:T(8,128)(2,1)S(1)}, u32[]{:S(2)}, u32[]{:S(2)}) collective-permute-start(bf16[912,128]{1,0:T(8,128)(2,1)S(1)} %fusion.11), channel_id=1, source_target_pairs={{1,17},{3,19},{5,21},{7,23},{9,25},{11,27},{13,29},{15,31},{16,0},... | collective-permute-start | bytes 700424 | tf_op jit(solution)/shard_map/ppermute | solution.py:393
  194.4 5.6 %collective-permute-start.19 = (bf16[384,128]{1,0:T(8,128)(2,1)S(1)}, bf16[384,128]{1,0:T(8,128)(2,1)S(1)}, u32[]{:S(2)}, u32[]{:S(2)}) collective-permute-start(bf16[384,128]{1,0:T(8,128)(2,1)S(1)} %fusion.13), channel_id=1, source_target_pairs={{0,16},{1,17},{2,18},{3,19},{4,20},{5,21},{6,22},{7,23},{8,24},{9,... | collective-permute-start | bytes 294920 | tf_op jit(solution)/shard_map/ppermute | solution.py:392
  194.5 7.7 %collective-permute-start.13 = (f32[19,24,128]{2,1,0:T(8,128)S(1)}, f32[19,24,128]{2,1,0:T(8,128)S(1)}, u32[]{:S(2)}, u32[]{:S(2)}) collective-permute-start(f32[19,24,128]{2,1,0:T(8,128)S(1)} %select_bitcast_fusion), channel_id=1, source_target_pairs={{0,1},{1,0},{2,3},{3,2},{4,5},{5,4},{6,7},{7,6},{8,9},{9,8},{10,11... | collective-permute-start | bytes 700424 | tf_op jit(solution)/shard_map/ppermute | solution.py:526
  200.0 1.4 collective-permute-start.20
  200.1 14.8 %collective-permute-start.17 = (bf16[1536,128]{1,0:T(8,128)(2,1)S(1)}, bf16[1536,128]{1,0:T(8,128)(2,1)S(1)}, u32[]{:S(2)}, u32[]{:S(2)}) collective-permute-start(bf16[1536,128]{1,0:T(8,128)(2,1)S(1)} %fusion.7), channel_id=1, source_target_pairs={{1,17},{3,19},{5,21},{7,23},{9,25},{11,27},{13,29},{15,31},{16,0},... | collective-permute-start | bytes 1179656 | tf_op jit(solution)/shard_map/ppermute | solution.py:393
  215.5 2.1 collective-permute-start.18

commit v2 on v1

--- a/solution.py
+++ b/solution.py
@@ -595,11 +595,670 @@
     return (block_out.reshape(seqs, half_tokens, width), input_grad.reshape(seqs, half_tokens, width), *summed)
 
 
+MESH = pl.DeviceIdType.MESH
+
+
+def bit(value, place):
+    return (value // (1 << place)) % 2
+
+
+def other_bit(a, b):
+    return a + b - 2 * a * b
+
+
+def layout_of(width, cols, ff):
+    low, wide = width // 16, ff // 8
+    table, row, final = {}, 0, 0
+    for name, kind, pieces, each in (
+        ("gate", "B", width // LANES, wide), ("up", "B", width // LANES, wide), ("down", "A", ff // LANES, low),
+        ("out", "A", cols // LANES, low), ("query", "B", width // LANES, low), ("key", "B", width // LANES, low),
+        ("value", "B", width // LANES, low), ("gains", "A", 1, low),
+    ):
+        rows = pieces * each * (2 if kind == "A" else 1)
+        table[name] = (row, rows, kind, pieces, each, final)
+        row, final = row + rows, final + pieces * each // 2
+    return table, row, final
+
+
+def block_kernel(
+    x_hbm, ids_hbm, dy_hbm, wq_hbm, wk_hbm, wv_hbm, wo_hbm, wg_hbm, wu_hbm, wd_hbm, gain_one, gain_two,
+    cos_f, sin_f, cos_c, sin_c,
+    block_out, input_grad, final_out,
+    xs, dys, ids, seg_col, wq, wk, wv, wo, wg, wu, wd, normed1, q_ref, k_ref, v_ref, att, att_other, lse_ref, bias_ref,
+    res_ref, normed2, hidden, d_gate, d_up, dn_own, dn_other, out_keep, out_send, out_got, dv_ref, dn_keep, dn_got,
+    gains, pack, got1, got2, got3, got4, acc, final, final_got,
+    load_sem, pair_send, pair_recv, hop_send, hop_recv,
+):
+    core = lax.axis_index("seq")
+    chip = lax.axis_index("dp")
+    half_tokens, width = x_hbm.shape
+    length = 2 * half_tokens
+    cols = wq.shape[1]
+    ff = wg.shape[1]
+    blocks = length // TB
+    half_blocks = half_tokens // TB
+    tables = (cos_f, sin_f, cos_c, sin_c)
+    chunks, _, _ = layout_of(width, cols, ff)
+    names = list(chunks)
+    low = width // 16
+
+    bx, by, bz, bw = (bit(chip, i) for i in range(4))
+    step_x, step_y = 1 - 2 * bx, 2 * (1 - 2 * by)
+    partners = (
+        chip + (1 - core) * step_x + core * step_y,
+        chip + core * step_x + (1 - core) * step_y,
+        chip + 4 * (1 - 2 * bz),
+        chip + 8 * (1 - 2 * bw),
+    )
+    holds = bw == core
+
+    def slot_of(owner):
+        kx, ky, kz = other_bit(bx, owner & 1), other_bit(by, (owner >> 1) & 1), other_bit(bz, (owner >> 2) & 1)
+        first = (1 - core) * kx + core * ky
+        second = core * kx + (1 - core) * ky
+        return first * 4 + second * 2 + kz, other_bit(bw, (owner >> 3) & 1)
+
+    def owner_of(first, second, third):
+        kx = (1 - core) * first + core * second
+        ky = core * first + (1 - core) * second
+        return other_bit(bx, kx) + 2 * other_bit(by, ky) + 4 * other_bit(bz, third)
+
+    barrier = pltpu.get_barrier_semaphore()
+    everyone = [{"dp": chip, "seq": 1 - core}] + [{"dp": p, "seq": core} for p in partners]
+    for device in everyone:
+        pl.semaphore_signal(barrier, inc=1, device_id=device, device_id_type=MESH)
+
+    own_rows = pl.ds(pl.multiple_of(core * half_tokens, half_tokens), half_tokens)
+    own_cols = pl.ds(pl.multiple_of(core * cols, cols), cols)
+    own_ff = pl.ds(pl.multiple_of(core * ff, ff), ff)
+
+    def load(i, src, dst):
+        return pltpu.make_async_copy(src, dst, load_sem.at[i])
+
+    loads = [
+        load(0, x_hbm, xs.at[own_rows]),
+        load(1, wv_hbm.at[:, own_cols], wv),
+        load(2, wq_hbm.at[:, own_cols], wq),
+        load(3, wk_hbm.at[:, own_cols], wk),
+        load(4, ids_hbm, ids.at[:, own_rows]),
+        load(5, wo_hbm, wo),
+        load(6, wg_hbm.at[:, own_ff], wg),
+        load(7, wu_hbm.at[:, own_ff], wu),
+        load(8, wd_hbm.at[own_ff, :], wd),
+        load(9, dy_hbm, dys.at[own_rows]),
+    ]
+    for copy in loads:
+        copy.start()
+
+    def to_pair(i, src, dst):
+        return pltpu.make_async_remote_copy(
+            src_ref=src, dst_ref=dst, send_sem=pair_send.at[i], recv_sem=pair_recv.at[i],
+            device_id={"dp": chip, "seq": 1 - core}, device_id_type=MESH,
+        )
+
+    send_x = to_pair(0, x_hbm, xs.at[own_rows])
+    send_ids = to_pair(1, ids_hbm, ids.at[:, own_rows])
+    send_dy = to_pair(2, dy_hbm, dys.at[own_rows])
+
+    def rows_of(t):
+        return pl.ds(pl.multiple_of(t * TB, TB), TB)
+
+    def send_att(t):
+        return to_pair(3 + t, att.at[rows_of(t)], att_other.at[rows_of(t)])
+
+    def send_dn(t):
+        return to_pair(7 + t, dn_own.at[rows_of(t)], dn_other.at[rows_of(t)])
+
+    def send_out(t):
+        return to_pair(11 + t, out_send.at[rows_of(t)], out_got.at[rows_of(t)])
+
+    def send_dn1(t):
+        return to_pair(13 + t, out_send.at[rows_of(t)], dn_got.at[rows_of(t)])
+
+    def write_out(t):
+        return pltpu.make_async_copy(out_got.at[rows_of(t)], block_out.at[rows_of(t)], load_sem.at[3 + t])
+
+    def write_grad(t):
+        return pltpu.make_async_copy(dn_got.at[rows_of(t)], input_grad.at[rows_of(t)], load_sem.at[5 + t])
+
+    def send_final(i, first, count):
+        rows = pl.ds(first, count)
+        return to_pair(15 + i, final.at[1 - core, rows], final_got.at[rows])
+
+
+    def hop(name, step):
+        row, count, kind = chunks[name][:3]
+        at = 4 * names.index(name) + step
+        rows = pl.ds(row, count)
+        if step < 3:
+            n = 4 >> step
+            src, dst = pack.at[pl.ds(n, n), rows], (got1, got2, got3)[step].at[:, rows]
+        elif kind == "B":
+            src, dst = pack.at[0, rows], got4.at[rows]
+        else:
+            src, dst = pack.at[0, pl.ds(row + count // 2, count // 2)], got4.at[pl.ds(row, count // 2)]
+        return pltpu.make_async_remote_copy(
+            src_ref=src, dst_ref=dst, send_sem=hop_send.at[at], recv_sem=hop_recv.at[at],
+            device_id={"dp": partners[step], "seq": core}, device_id_type=MESH,
+        )
+
+    def start(name, step):
+        if step == 3 and chunks[name][2] == "B":
+            @pl.when(jnp.logical_not(holds))
+            def _():
+                hop(name, step).start()
+        else:
+            hop(name, step).start()
+
+    def advance(name, step):
+        row, count, kind, pieces, each, at = chunks[name]
+        if step < 3:
+            hop(name, step).wait_recv()
+            n = 4 >> step
+            size = 384 if count % 384 == 0 else (288 if count % 288 == 0 else count)
+            source = (got1, got2, got3)[step]
+            per = count // size
+
+            def add(i, carry):
+                slab = i // per
+                rows = pl.ds(pl.multiple_of(row + (i % per) * size, 16), size)
+                total = pack[slab, rows, :].astype(F32) + source[slab, rows, :].astype(F32)
+                pack[slab, rows, :] = total.astype(BF)
+                if step == 2:
+                    acc[rows, :] = total
+                return carry
+
+            lax.fori_loop(0, n * per, add, 0)
+            start(name, step + 1)
+            return
+        half = each // 2
+        if kind == "B":
+            @pl.when(holds)
+            def _():
+                hop(name, step).wait_recv()
+                for p in range(pieces):
+                    for c in range(2):
+                        rows = pl.ds(row + p * each + c * half, half)
+                        final[c, pl.ds(at + p * half, half), :] = acc[rows, :] + got4[rows, :].astype(F32)
+
+            @pl.when(jnp.logical_not(holds))
+            def _():
+                hop(name, step).wait_send()
+                for p in range(pieces):
+                    for c in range(2):
+                        final[c, pl.ds(at + p * half, half), :] = acc[pl.ds(row + p * each + c * half, half), :]
+        else:
+            hop(name, step).wait_recv()
+            for p in range(pieces):
+                for c in range(2):
+                    rows = pl.ds(row + p * each + c * half, half)
+                    final[c, pl.ds(at + p * half, half), :] = acc[rows, :] + got4[rows, :].astype(F32)
+
+    def drain(name):
+        for step in range(3):
+            hop(name, step).wait_send()
+        if chunks[name][2] == "A":
+            hop(name, 3).wait_send()
+
+
+    pl.semaphore_wait(barrier, len(everyone))
+    send_x.start()
+    send_ids.start()
+    send_dy.start()
+    for copy in loads[:4]:
+        copy.wait()
+
+    def project(j, carry):
+        t = (core * half_blocks + j) % blocks
+
+        @pl.when(j == half_blocks)
+        def _():
+            send_x.wait_recv()
+
+        rows = rows_of(t)
+        x = xs[rows, :].astype(F32)
+        r = lax.rsqrt(jnp.mean(x * x, axis=-1, keepdims=True) + EPS)
+        normed = (x * r * gain_one[...]).astype(BF)
+        normed1[rows, :] = normed
+        v_ref[rows, :] = nn(normed, wv[...]).astype(BF)
+        q = nn(normed, wq[...]).astype(BF).astype(F32)
+        k = nn(normed, wk[...]).astype(BF).astype(F32)
+        for sub in range(TB // 64):
+            cosine, sine, low_half = angle_block(tables, t * (TB // 64) + sub)
+            at = pl.ds(pl.multiple_of(t * TB + sub * 64, 64), 64)
+            for tile in range(cols // LANES):
+                lanes = slice(tile * LANES, (tile + 1) * LANES)
+                part = slice(sub * 64, (sub + 1) * 64)
+                q_ref[at, lanes] = (rotate(q[part, lanes], cosine, sine, low_half).astype(BF) * BF(SCALE)).astype(BF)
+                k_ref[at, lanes] = rotate(k[part, lanes], cosine, sine, low_half).astype(BF)
+        return carry
+
+    lax.fori_loop(0, blocks, project, 0)
+    loads[4].wait()
+    send_ids.wait_recv()
+    seg_col[...] = jnp.transpose(jnp.broadcast_to(ids[...].astype(F32), (LANES, length)))
+
+    def set_bias(block):
+        first = window(block)
+        keys = (block + 1) * TB - first
+        rows = seg_col[pl.ds(block * TB, TB), 0:1]
+        columns = ids[:, pl.ds(first, keys)].astype(F32)
+        q_at = block * TB + lax.broadcasted_iota(jnp.int32, (TB, keys), 0)
+        k_at = first + lax.broadcasted_iota(jnp.int32, (TB, keys), 1)
+        bias_ref[:, :keys] = jnp.where((rows == columns) & (k_at <= q_at), 0.0, NEG).astype(F32)
+
+    lane = lax.broadcasted_iota(jnp.int32, (1, LANES), 1)
+    for block in range(blocks):
+        first = window(block)
+        keys = (block + 1) * TB - first
+        set_bias(block)
+        rows = pl.ds(block * TB, TB)
+        span = pl.ds(first, keys)
+
+        def head(h, carry, rows=rows, span=span, keys=keys):
+            lanes = pl.ds(pl.multiple_of((h // 2) * LANES, LANES), LANES)
+            mine = (lane // HD) == (h % 2)
+            q = q_ref[rows, lanes]
+            qm = jnp.where(mine, q, jnp.zeros_like(q))
+            scores = nt(qm, k_ref[span, lanes]) + bias_ref[:, :keys]
+            peak = jnp.max(scores, axis=-1, keepdims=True)
+            weights = jnp.exp(scores - peak)
+            total = jnp.sum(weights, axis=-1, keepdims=True)
+            probs = (weights * (1.0 / total)).astype(BF)
+            result = nn(probs, v_ref[span, lanes]).astype(BF)
+            att[rows, lanes] = jnp.where(mine, result, att[rows, lanes])
+            lse_ref[rows, :] = jnp.where(lane == h, peak + jnp.log(total), lse_ref[rows, :])
+            return carry
+
+        lax.fori_loop(0, cols // HD, head, 0)
+        send_att(block).start()
+
+
+    for copy in loads[5:]:
+        copy.wait()
+    send_dy.wait_recv()
+    other_cols = pl.ds(pl.multiple_of((1 - core) * cols, cols), cols)
+
+    def feed(t, carry):
+        rows = rows_of(t)
+        local = rows_of(t % half_blocks)
+        is_own = t // half_blocks == core
+        send_att(t).wait_recv()
+        x = xs[rows, :].astype(F32)
+        dy = dys[rows, :]
+        residual = x + (nn(att[rows, :], wo[own_cols, :]) + nn(att_other[rows, :], wo[other_cols, :]))
+        res_ref[rows, :] = residual
+        r = lax.rsqrt(jnp.mean(residual * residual, axis=-1, keepdims=True) + EPS)
+        n2 = (residual * r * gain_two[...]).astype(BF)
+        normed2[rows, :] = n2
+        gate = nn(n2, wg[...])
+        up = nn(n2, wu[...])
+        sig = 1.0 / (1.0 + jnp.exp(-gate))
+        act = gate * sig
+        hid = (act * up).astype(BF)
+        hidden[rows, :] = hid
+        d_hidden = nt(dy, wd[...])
+        dg = (d_hidden * up * (sig * (1.0 + gate * (1.0 - sig)))).astype(BF)
+        du = (d_hidden * act).astype(BF)
+        d_gate[rows, :] = dg
+        d_up[rows, :] = du
+        dn_own[rows, :] = (nt(dg, wg[...]) + nt(du, wu[...])).astype(BF)
+        send_dn(t).start()
+        down = nn(hid, wd[...])
+
+        @pl.when(is_own)
+        def _():
+            out_keep[local, :] = residual + down
+
+        @pl.when(jnp.logical_not(is_own))
+        def _():
+            out_send[local, :] = down.astype(BF)
+            send_out(t % half_blocks).start()
+
+        return carry
+
+    lax.fori_loop(0, blocks, feed, 0)
+
+    wide = ff // 8
+    pieces = width // LANES
+
+    def gate_up(name, source, first):
+        row = chunks[name][0]
+
+        def slot(j, carry):
+            owner = owner_of(first, j // 2, j % 2)
+            cut = pl.ds(pl.multiple_of(owner * wide, wide), wide)
+            grad = tn(source[:, cut], normed2[...]).astype(BF)
+            for piece in range(pieces):
+                pack[4 * first + j, pl.ds(row + piece * wide, wide), :] = grad[:, piece * LANES : (piece + 1) * LANES]
+            return carry
+
+        lax.fori_loop(0, 4, slot, 0)
+
+    gate_up("gate", d_gate, 1)
+    start("gate", 0)
+    gate_up("gate", d_gate, 0)
+    gate_up("up", d_up, 1)
+    start("up", 0)
+    gate_up("up", d_up, 0)
+
+    def spread(name, piece, grad, count):
+        row, rows = chunks[name][:2]
+        for o in range(16):
+            slot, far = slot_of(o)
+            at = pl.multiple_of(row + far * (rows // 2) + piece * low, 16)
+            pack[slot, pl.ds(at, low), :] = grad[o * low : (o + 1) * low, :]
+
+    def down_piece(piece, carry):
+        lanes = pl.ds(pl.multiple_of(piece * LANES, LANES), LANES)
+        spread("down", piece, tn(dys[...], hidden[:, lanes]).astype(BF), 8)
+        return carry
+
+    lax.fori_loop(0, ff // LANES, down_piece, 0)
+    start("down", 0)
+    advance("gate", 0)
+
+
+    d_branch, d_att = normed2, hidden
+    gains[...] = jnp.zeros_like(gains)
+
+    def norm_two(t, carry):
+        rows = rows_of(t)
+        local = rows_of(t % half_blocks)
+        is_own = t // half_blocks == core
+        send_dn(t).wait_recv()
+        dy = dys[rows, :].astype(F32)
+        residual = res_ref[rows, :]
+        dn = dn_own[rows, :].astype(F32) + dn_other[rows, :].astype(F32)
+        r = lax.rsqrt(jnp.mean(residual * residual, axis=-1, keepdims=True) + EPS)
+        scaled = residual * r
+        e = gain_two[...] * dn
+        grad = dy + r * (e - scaled * (r * jnp.mean(e * residual, axis=-1, keepdims=True)))
+        small = grad.astype(BF)
+        d_branch[rows, :] = small
+        d_att[rows, 0:cols] = nt(small, wo[own_cols, :]).astype(BF)
+
+        @pl.when(is_own)
+        def _():
+            gains[0:1, :] += jnp.sum(dn * scaled, axis=0, keepdims=True)
+            send_out(t % half_blocks).wait_recv()
+            out_got[local, :] = (out_keep[local, :] + out_got[local, :].astype(F32)).astype(BF)
+            write_out(t % half_blocks).start()
+            out_keep[local, :] = grad
+
+        return carry
+
+    lax.fori_loop(0, blocks, norm_two, 0)
+    d_res = out_keep
+
+    def out_piece(piece, carry):
+        lanes = pl.ds(pl.multiple_of(piece * LANES, LANES), LANES)
+        spread("out", piece, tn(d_branch[...], att[:, lanes]).astype(BF), 3)
+        return carry
+
+    lax.fori_loop(0, cols // LANES, out_piece, 0)
+    start("out", 0)
+
+    res_ref[:, cols:] = jnp.zeros((length, cols), F32)
+    dv_ref[...] = jnp.zeros_like(dv_ref)
+
+    def attention_back(block, first_head, last_head):
+        first = window(block)
+        keys = (block + 1) * TB - first
+        rows = pl.ds(block * TB, TB)
+        span = pl.ds(first, keys)
+
+        def head(h, carry):
+            at = pl.multiple_of((h // 2) * LANES, LANES)
+            lanes = pl.ds(at, LANES)
+            k_lanes = pl.ds(pl.multiple_of(cols + at, LANES), LANES)
+            mine = (lane // HD) == (h % 2)
+            q = q_ref[rows, lanes]
+            qm = jnp.where(mine, q, jnp.zeros_like(q))
+            do = d_att[rows, lanes]
+            dom = jnp.where(mine, do, jnp.zeros_like(do))
+            lse = jnp.sum(jnp.where(lane == h, lse_ref[rows, :], 0.0), axis=-1, keepdims=True)
+            k = k_ref[span, lanes]
+            probs = jnp.exp(nt(qm, k) + (bias_ref[:, :keys] - lse))
+            d_probs = nt(dom, v_ref[span, lanes])
+            delta = jnp.sum(probs * d_probs, axis=-1, keepdims=True)
+            ds = (probs * (d_probs - delta)).astype(BF)
+            res_ref[rows, lanes] = jnp.where(mine, nn(ds, k), res_ref[rows, lanes])
+            res_ref[span, k_lanes] += tn(ds, qm)
+            dv_ref[span, lanes] += tn(probs.astype(BF), dom)
+            return carry
+
+        lax.fori_loop(first_head, last_head, head, 0)
+
+    heads = cols // HD
+    progress = {
+        (0, 0): [("up", 0)],
+        (1, 0): [("gate", 1)],
+        (1, 1): [("down", 0)],
+        (2, 0): [("up", 1), ("gate", 2)],
+        (2, 1): [("out", 0), ("down", 1)],
+        (3, 0): [("up", 2), ("out", 1)],
+        (3, 1): [("down", 2), ("gate", 3)],
+    }
+    for block in range(blocks):
+        set_bias(block)
+        for part in range(2):
+            attention_back(block, part * heads // 2, (part + 1) * heads // 2)
+            for name, step in progress.get((block, part), ()):
+                advance(name, step)
+
+    def lower(t, carry):
+        rows = rows_of(t)
+        for sub in range(TB // 64):
+            cosine, sine, low_half = angle_block(tables, t * (TB // 64) + sub)
+            at = pl.ds(pl.multiple_of(t * TB + sub * 64, 64), 64)
+            for tile in range(cols // LANES):
+                lanes = slice(tile * LANES, (tile + 1) * LANES)
+                k_lanes = slice(cols + tile * LANES, cols + (tile + 1) * LANES)
+                d_gate[at, lanes] = (rotate(res_ref[at, lanes], cosine, -sine, low_half) * SCALE).astype(BF)
+                d_gate[at, k_lanes] = rotate(res_ref[at, k_lanes], cosine, -sine, low_half).astype(BF)
+        d_up[rows, 0:cols] = dv_ref[rows, :].astype(BF)
+        return carry
+
+    lax.fori_loop(0, blocks, lower, 0)
+
+    def qkv(name, source, lanes_at):
+        row = chunks[name][0]
+
+        def piece_of(piece, carry):
+            lanes = pl.ds(pl.multiple_of(piece * LANES, LANES), LANES)
+            grad = tn(source[:, lanes_at : lanes_at + cols], normed1[:, lanes]).astype(BF)
+            for o in range(8):
+                at = pl.multiple_of(row + piece * low, 16)
+                pack[slot_of(o)[0], pl.ds(at, low), :] = grad[o * low : (o + 1) * low, :]
+            return carry
+
+        lax.fori_loop(0, pieces, piece_of, 0)
+        start(name, 0)
+
+    qkv("value", d_up, 0)
+    qkv("query", d_gate, 0)
+    qkv("key", d_gate, cols)
+    advance("up", 3)
+    advance("out", 2)
+
+    def finish(j, carry):
+        t = ((1 - core) * half_blocks + j) % blocks
+        rows = rows_of(t)
+        local = rows_of(t % half_blocks)
+        is_own = t // half_blocks == core
+        dn = nt(d_gate[rows, 0:cols], wq[...]) + nt(d_gate[rows, cols : 2 * cols], wk[...]) + nt(d_up[rows, 0:cols], wv[...])
+        x = xs[rows, :].astype(F32)
+        r = lax.rsqrt(jnp.mean(x * x, axis=-1, keepdims=True) + EPS)
+        gains[1:2, :] += jnp.sum(dn * (x * r), axis=0, keepdims=True)
+
+        @pl.when(is_own)
+        def _():
+            dn_keep[local, :] = dn
+
+        @pl.when(jnp.logical_not(is_own))
+        def _():
+            send_out(t % half_blocks).wait_send()
+            out_send[local, :] = dn.astype(BF)
+            send_dn1(t % half_blocks).start()
+
+        return carry
+
+    lax.fori_loop(0, blocks, finish, 0)
+    turned = jnp.transpose(gains[...])
+    turned_low = turned.astype(BF)
+    rest = turned - turned_low.astype(F32)
+    both = jnp.where(lane < LANES // 2, turned, pltpu.roll(rest, LANES // 2, 1)).astype(BF)
+    spread("gains", 0, both, 1)
+    start("gains", 0)
+    advance("value", 0)
+
+    def input_part(t, carry):
+        local = rows_of(t)
+        send_dn1(t).wait_recv()
+        dn = dn_keep[local, :] + dn_got[local, :].astype(F32)
+        x = xs[rows_of(core * half_blocks + t), :].astype(F32)
+        r = lax.rsqrt(jnp.mean(x * x, axis=-1, keepdims=True) + EPS)
+        e = gain_one[...] * dn
+        grad = d_res[local, :] + r * e - x * (r * r * r) * jnp.mean(e * x, axis=-1, keepdims=True)
+        dn_got[local, :] = grad.astype(BF)
+        write_grad(t).start()
+        return carry
+
+    lax.fori_loop(0, half_blocks, input_part, 0)
+    advance("query", 0)
+    advance("value", 1)
+    advance("down", 3)
+    advance("out", 3)
+    early = chunks["query"][5]
+    send_final(0, 0, early).start()
+    advance("key", 0)
+    advance("query", 1)
+    advance("value", 2)
+    advance("gains", 0)
+    advance("key", 1)
+    advance("query", 2)
+    advance("gains", 1)
+    advance("key", 2)
+    advance("gains", 2)
+    advance("value", 3)
+    advance("query", 3)
+    advance("key", 3)
+    advance("gains", 3)
+    rows_final = final.shape[1]
+    send_final(1, early, rows_final - early).start()
+    mine_out = load(0, final.at[core], final_out.at[0])
+    mine_out.start()
+    send_final(0, 0, early).wait_recv()
+    early_out = load(1, final_got.at[pl.ds(0, early)], final_out.at[1, pl.ds(0, early)])
+    early_out.start()
+    for name in names:
+        drain(name)
+    send_x.wait_send()
+    send_ids.wait_send()
+    send_dy.wait_send()
+    for t in range(blocks):
+        send_att(t).wait_send()
+        send_dn(t).wait_send()
+    for t in range(half_blocks):
+        write_out(t).wait()
+        write_grad(t).wait()
+        send_dn1(t).wait_send()
+    send_final(0, 0, early).wait_send()
+    send_final(1, early, rows_final - early).wait()
+    late = pl.ds(early, rows_final - early)
+    late_out = load(2, final_got.at[late], final_out.at[1, late])
+    late_out.start()
+    mine_out.wait()
+    early_out.wait()
+    late_out.wait()
+
+
+def fused_shards(
+    tokens, segment_ids, norm1_gain, w_query, w_key, w_value, w_out, norm2_gain, w_gate, w_up, w_down, out_grad,
+):
+    seqs, half_tokens, width = tokens.shape
+    length = 2 * half_tokens
+    cols = w_query.shape[1] // 2
+    ff = w_gate.shape[1] // 2
+    chunks, rows, rows_final = layout_of(width, cols, ff)
+    core = lax.axis_index("seq")
+    chip = lax.axis_index("dp")
+    tables = tuple(jnp.asarray(t) for t in small_tables(length))
+    any_space = pl.BlockSpec(memory_space=pl.ANY)
+    vmem = pl.BlockSpec(memory_space=pltpu.VMEM)
+
+    def low(*dims):
+        return pltpu.VMEM(dims, BF)
+
+    def full(*dims):
+        return pltpu.VMEM(dims, F32)
+
+    scratch = [
+        low(length, width), low(length, width), pltpu.VMEM((1, length), jnp.int32), full(length, LANES),
+        low(width, cols), low(width, cols), low(width, cols), low(width, width), low(width, ff), low(width, ff), low(ff, width),
+        low(length, width), low(length, cols), low(length, cols), low(length, cols), low(length, cols), low(length, cols),
+        full(length, LANES), full(TB, 3 * TB),
+        full(length, width), low(length, width), low(length, ff), low(length, ff), low(length, ff), low(length, width),
+        low(length, width), full(half_tokens, width), low(half_tokens, width), low(half_tokens, width), full(length, cols),
+        full(half_tokens, width), low(half_tokens, width),
+        full(LANES, width), low(8, rows, LANES), low(4, rows, LANES), low(2, rows, LANES), low(1, rows, LANES), low(rows, LANES),
+        full(rows, LANES), full(2, rows_final, LANES), full(rows_final, LANES),
+        pltpu.SemaphoreType.DMA((10,)), pltpu.SemaphoreType.DMA((17,)), pltpu.SemaphoreType.DMA((17,)),
+        pltpu.SemaphoreType.DMA((4 * len(chunks),)), pltpu.SemaphoreType.DMA((4 * len(chunks),)),
+    ]
+    block_out, input_grad, final = pl.pallas_call(
+        block_kernel,
+        out_shape=(shape(half_tokens, width), shape(half_tokens, width), shape(2, rows_final, LANES, dtype=F32)),
+        in_specs=[any_space] * 10 + [vmem] * 6,
+        out_specs=[any_space] * 3,
+        scratch_shapes=scratch,
+        compiler_params=pltpu.CompilerParams(
+            vmem_limit_bytes=67043328, collective_id=0, has_side_effects=True,
+        ),
+        name="block",
+    )(
+        tokens.reshape(half_tokens, width), segment_ids.reshape(1, half_tokens), out_grad.reshape(half_tokens, width),
+        w_query, w_key, w_value, w_out, w_gate, w_up, w_down,
+        norm1_gain.astype(F32).reshape(1, width), norm2_gain.astype(F32).reshape(1, width), *tables,
+    )
+    mine, got = final[0], final[1]
+    holds = (chip >> 3) == core
+
+    def part(name):
+        _, _, kind, pieces, each, at = chunks[name]
+        half = each // 2
+        cut = slice(at, at + pieces * half)
+        a, b = mine[cut].reshape(pieces, half, LANES), got[cut].reshape(pieces, half, LANES)
+        if kind == "B":
+            taken = jnp.where(holds, a, b)
+        else:
+            taken = jnp.where(core == 0, jnp.concatenate([a, b]), jnp.concatenate([b, a]))
+        return jnp.transpose(taken, (0, 2, 1)).reshape(-1, half)
+
+    gains = part("gains")
+    gains = gains[:LANES] + gains[LANES:]
+    summed = (
+        gains[1] + gains[1 + LANES // 2],
+        part("query"),
+        part("key"),
+        part("value"),
+        part("out"),
+        gains[0] + gains[LANES // 2],
+        part("gate"),
+        part("up"),
+        part("down"),
+    )
+    return (block_out.reshape(seqs, half_tokens, width), input_grad.reshape(seqs, half_tokens, width), *summed)
+
+
 def solution(mesh):
     placed = (P("dp", "seq", None), P("dp", "seq"), *([P()] * 9), P("dp", "seq", None))
     column = P(None, AX)
+    chips = mesh.shape["dp"]
+    body = fused_shards if chips == 16 else functools.partial(shards, chips=chips)
     return jax.shard_map(
-        functools.partial(shards, chips=mesh.shape["dp"]),
+        body,
         mesh=mesh,
         in_specs=placed,
         out_specs=(

time: 219 us -> 147 us (0.67)
  waiting for transfers between devices: 64.2 us -> 0 us
  Pallas kernels: 103 us -> 134 us
  starting transfers between devices: 19.3 us -> 0 us
  other arithmetic: 16.9 us -> 2.25 us
  local copies, waits for them, and re-layouts: 14.4 us -> 9.41 us
    ppermute x21 -> x0, waiting for transfers between devices: 64.2 us -> none  [the longest x6 37.1 us: halve(): got = lax.ppermute(pack3[1], AX, swap_chips(step))]
    pallas_call x3 -> x1, Pallas kernels: 103 us -> 134 us  [fused_shards(): pl.pallas_call(block_kernel, out_shape=(shape(half_tokens, width), shape(...]
    ppermute x21 -> x0, starting transfers between devices: 19.3 us -> none  [the longest x6 10 us: halve(): got = lax.ppermute(pack3[1], AX, swap_chips(step))]
    convert_element_type x5 -> x0, other arithmetic: 4.69 us -> none  [the longest x4 4.69 us: halve(): pack = total.astype(BF) if step < 2 else total]
    select_n x12 -> x3, other arithmetic: 4.37 us -> 0.11 us  [the longest x2 0.06 us: part(): taken = jnp.where(holds, a, b)]
    reshape x3 -> x1, other arithmetic: 4.65 us -> 0.69 us  [part(): return jnp.transpose(taken, (0, 2, 1)).reshape(-1, half)]
    slice x9 -> x3, local copies, waits for them, and re-layouts: 6.21 us -> 2.59 us  [the longest x2 1.75 us: part(): mine[cut].reshape(pieces, half, LANES)]
    reshape x5 -> x7, local copies, waits for them, and re-layouts: 3.96 us -> 4.74 us  [the longest x3 2.19 us: part(): return jnp.transpose(taken, (0, 2, 1)).reshape(-1, half)]
  transfers between devices with their start and end apart: 21 -> 0, of which waited for: 11 -> 0; matrix products, arithmetic and copies ran while one was open for 10% -> 0% of each run, Pallas kernels for 31% -> 0%
where the time goes in v2:
time: 147 us; the launch traced here: 146 us
  Pallas kernels  134 us (91%)
  local copies, waits for them, and re-layouts  9.41 us (6%)
  other arithmetic  2.25 us (2%)
    pallas_call x1, Pallas kernels, fused_shards(): pl.pallas_call(block_kernel, out_shape=(shape(half_tokens, width), shape(...  134 us

profile of v2, /device:TPU:0, one launch (start us, length us, event | category | flops | bytes accessed | tf_op | source)
XLA Modules:
  0.0 146.4 jit_solution(3717686954483142047)
XLA Ops:
  0.7 1.3 reshape.165.gain_one
  1.9 1.3 reshape.167.gain_two
  3.2 134.0 %block.1 = (bf16[512,768]{1,0:T(8,128)(2,1)}, bf16[512,768]{1,0:T(8,128)(2,1)}, f32[2,1488,128]{2,1,0:T(8,128)}) custom-call(bf16[512,768]{1,0:T(8,128)(2,1)} %bitcast.59, s32[1,512]{1,0:T(1,128)} %ids_hbm.1, bf16[512,768]{1,0:T(8,128)(2,1)} %bitcast.60, bf16[768,768]{1,0:T(8,128)(2,1)} %wq_hbm.1, bf16[768,768]{1,0:T(8,128)(2,1)} %wk_hbm.1, ...), custom_call_target="tpu_custom_call" | custom-call | tf_op jit(solution)/shard_map/block/pallas_call | solution.py:1210
  137.1 0.0 copy-start
  137.2 0.8 fusion.6
  138.0 0.7 fusion.1
  138.7 0.7 fusion.2
  139.5 0.8 fusion.5
  140.3 1.0 fusion.4
  141.3 0.7 copy_bitcast_fusion.2
  142.0 0.0 copy-done
  142.1 0.0 copy-start.2
  142.1 0.7 copy_bitcast_fusion.3
  142.8 0.1 copy.41
  142.9 0.1 copy.42
  143.1 0.0 copy-start.1
  143.1 0.8 copy_bitcast_fusion
  143.9 0.7 copy_bitcast_fusion.5
  144.6 0.0 copy-done.2
  144.6 0.9 copy.60
  145.5 0.0 copy-done.1
  145.5 0.9 copy.61
  (9 shorter events, 0.2 us)
Async XLA Ops:
  137.1 4.8 %copy-start = (f32[2,1488,128]{2,1,0:T(8,128)S(1)}, f32[2,1488,128]{2,1,0:T(8,128)}, u32[]{:S(2)}) copy-start(f32[2,1488,128]{2,1,0:T(8,128)} %get-tuple-element.16) | copy-start | bytes 4571140
  142.1 2.5 %copy-start.2 = (bf16[512,768]{1,0:T(8,128)(2,1)S(1)}, bf16[512,768]{1,0:T(8,128)(2,1)}, u32[]{:S(2)}) copy-start(bf16[512,768]{1,0:T(8,128)(2,1)} %get-tuple-element.14) | copy-start | bytes 2359300
  143.1 2.4 %copy-start.1 = (bf16[512,768]{1,0:T(8,128)(2,1)S(1)}, bf16[512,768]{1,0:T(8,128)(2,1)}, u32[]{:S(2)}) copy-start(bf16[512,768]{1,0:T(8,128)(2,1)} %get-tuple-element.15) | copy-start | bytes 2359300

commit v3 on v2

--- a/solution.py
+++ b/solution.py
@@ -624,7 +624,7 @@
     x_hbm, ids_hbm, dy_hbm, wq_hbm, wk_hbm, wv_hbm, wo_hbm, wg_hbm, wu_hbm, wd_hbm, gain_one, gain_two,
     cos_f, sin_f, cos_c, sin_c,
     block_out, input_grad, final_out,
-    xs, dys, ids, seg_col, wq, wk, wv, wo, wg, wu, wd, normed1, q_ref, k_ref, v_ref, att, att_other, lse_ref, bias_ref,
+    xs, dys, ids, wq, wk, wv, wo, wg, wu, wd, normed1, q_ref, k_ref, v_ref, att, att_other, lse_ref, bias_ref,
     res_ref, normed2, hidden, d_gate, d_up, dn_own, dn_other, out_keep, out_send, out_got, dv_ref, dn_keep, dn_got,
     gains, pack, got1, got2, got3, got4, acc, final, final_got,
     load_sem, pair_send, pair_recv, hop_send, hop_recv,
@@ -836,18 +836,19 @@
     lax.fori_loop(0, blocks, project, 0)
     loads[4].wait()
     send_ids.wait_recv()
-    seg_col[...] = jnp.transpose(jnp.broadcast_to(ids[...].astype(F32), (LANES, length)))
+    lse_ref[...] = jnp.transpose(jnp.broadcast_to(ids[...].astype(F32), (LANES, length)))
 
     def set_bias(block):
         first = window(block)
         keys = (block + 1) * TB - first
-        rows = seg_col[pl.ds(block * TB, TB), 0:1]
+        rows = lse_ref[pl.ds(block * TB, TB), LANES - 1 :]
         columns = ids[:, pl.ds(first, keys)].astype(F32)
         q_at = block * TB + lax.broadcasted_iota(jnp.int32, (TB, keys), 0)
         k_at = first + lax.broadcasted_iota(jnp.int32, (TB, keys), 1)
         bias_ref[:, :keys] = jnp.where((rows == columns) & (k_at <= q_at), 0.0, NEG).astype(F32)
 
     lane = lax.broadcasted_iota(jnp.int32, (1, LANES), 1)
+    first_head = lane < HD
     for block in range(blocks):
         first = window(block)
         keys = (block + 1) * TB - first
@@ -855,22 +856,23 @@
         rows = pl.ds(block * TB, TB)
         span = pl.ds(first, keys)
 
-        def head(h, carry, rows=rows, span=span, keys=keys):
-            lanes = pl.ds(pl.multiple_of((h // 2) * LANES, LANES), LANES)
-            mine = (lane // HD) == (h % 2)
-            q = q_ref[rows, lanes]
-            qm = jnp.where(mine, q, jnp.zeros_like(q))
-            scores = nt(qm, k_ref[span, lanes]) + bias_ref[:, :keys]
-            peak = jnp.max(scores, axis=-1, keepdims=True)
-            weights = jnp.exp(scores - peak)
-            total = jnp.sum(weights, axis=-1, keepdims=True)
-            probs = (weights * (1.0 / total)).astype(BF)
-            result = nn(probs, v_ref[span, lanes]).astype(BF)
-            att[rows, lanes] = jnp.where(mine, result, att[rows, lanes])
-            lse_ref[rows, :] = jnp.where(lane == h, peak + jnp.log(total), lse_ref[rows, :])
+        def pair(j, carry, rows=rows, span=span, keys=keys):
+            lanes = pl.ds(pl.multiple_of(j * LANES, LANES), LANES)
+            q, k, v = q_ref[rows, lanes], k_ref[span, lanes], v_ref[span, lanes]
+            results, sums = [], []
+            for mine in (first_head, jnp.logical_not(first_head)):
+                scores = nt(jnp.where(mine, q, jnp.zeros_like(q)), k) + bias_ref[:, :keys]
+                peak = jnp.max(scores, axis=-1, keepdims=True)
+                weights = jnp.exp(scores - peak)
+                total = jnp.sum(weights, axis=-1, keepdims=True)
+                results.append(nn(weights.astype(BF), v) * (1.0 / total))
+                sums.append(peak + jnp.log(total))
+            att[rows, lanes] = jnp.where(first_head, *results).astype(BF)
+            old = jnp.where(lane == 2 * j + 1, sums[1], lse_ref[rows, :])
+            lse_ref[rows, :] = jnp.where(lane == 2 * j, sums[0], old)
             return carry
 
-        lax.fori_loop(0, cols // HD, head, 0)
+        lax.fori_loop(0, cols // LANES, pair, 0)
         send_att(block).start()
 
 
@@ -925,15 +927,15 @@
     def gate_up(name, source, first):
         row = chunks[name][0]
 
-        def slot(j, carry):
+        cuts = []
+        for j in range(4):
             owner = owner_of(first, j // 2, j % 2)
-            cut = pl.ds(pl.multiple_of(owner * wide, wide), wide)
-            grad = tn(source[:, cut], normed2[...]).astype(BF)
+            cuts.append(source[:, pl.ds(pl.multiple_of(owner * wide, wide), wide)])
+        grad = tn(jnp.concatenate(cuts, axis=1), normed2[...]).astype(BF)
+        for j in range(4):
             for piece in range(pieces):
-                pack[4 * first + j, pl.ds(row + piece * wide, wide), :] = grad[:, piece * LANES : (piece + 1) * LANES]
-            return carry
-
-        lax.fori_loop(0, 4, slot, 0)
+                part = grad[j * wide : (j + 1) * wide, piece * LANES : (piece + 1) * LANES]
+                pack[4 * first + j, pl.ds(row + piece * wide, wide), :] = part
 
     gate_up("gate", d_gate, 1)
     start("gate", 0)
@@ -942,19 +944,21 @@
     start("up", 0)
     gate_up("up", d_up, 0)
 
-    def spread(name, piece, grad, count):
+    def spread(name, piece, grad):
         row, rows = chunks[name][:2]
         for o in range(16):
             slot, far = slot_of(o)
             at = pl.multiple_of(row + far * (rows // 2) + piece * low, 16)
             pack[slot, pl.ds(at, low), :] = grad[o * low : (o + 1) * low, :]
 
-    def down_piece(piece, carry):
-        lanes = pl.ds(pl.multiple_of(piece * LANES, LANES), LANES)
-        spread("down", piece, tn(dys[...], hidden[:, lanes]).astype(BF), 8)
+    def down_part(part, carry):
+        at = part * (ff // 2)
+        grad = tn(dys[...], hidden[:, pl.ds(pl.multiple_of(at, LANES), ff // 2)]).astype(BF)
+        for piece in range(ff // 2 // LANES):
+            spread("down", part * (ff // 2 // LANES) + piece, grad[:, piece * LANES : (piece + 1) * LANES])
         return carry
 
-    lax.fori_loop(0, ff // LANES, down_piece, 0)
+    lax.fori_loop(0, 2, down_part, 0)
     start("down", 0)
     advance("gate", 0)
 
@@ -991,46 +995,45 @@
     lax.fori_loop(0, blocks, norm_two, 0)
     d_res = out_keep
 
-    def out_piece(piece, carry):
-        lanes = pl.ds(pl.multiple_of(piece * LANES, LANES), LANES)
-        spread("out", piece, tn(d_branch[...], att[:, lanes]).astype(BF), 3)
-        return carry
-
-    lax.fori_loop(0, cols // LANES, out_piece, 0)
+    out_grad = tn(d_branch[...], att[...]).astype(BF)
+    for piece in range(cols // LANES):
+        spread("out", piece, out_grad[:, piece * LANES : (piece + 1) * LANES])
     start("out", 0)
 
     res_ref[:, cols:] = jnp.zeros((length, cols), F32)
     dv_ref[...] = jnp.zeros_like(dv_ref)
 
-    def attention_back(block, first_head, last_head):
+    def attention_back(block, first_pair, last_pair):
         first = window(block)
         keys = (block + 1) * TB - first
         rows = pl.ds(block * TB, TB)
         span = pl.ds(first, keys)
 
-        def head(h, carry):
-            at = pl.multiple_of((h // 2) * LANES, LANES)
+        def pair(j, carry):
+            at = pl.multiple_of(j * LANES, LANES)
             lanes = pl.ds(at, LANES)
             k_lanes = pl.ds(pl.multiple_of(cols + at, LANES), LANES)
-            mine = (lane // HD) == (h % 2)
-            q = q_ref[rows, lanes]
-            qm = jnp.where(mine, q, jnp.zeros_like(q))
-            do = d_att[rows, lanes]
-            dom = jnp.where(mine, do, jnp.zeros_like(do))
-            lse = jnp.sum(jnp.where(lane == h, lse_ref[rows, :], 0.0), axis=-1, keepdims=True)
-            k = k_ref[span, lanes]
-            probs = jnp.exp(nt(qm, k) + (bias_ref[:, :keys] - lse))
-            d_probs = nt(dom, v_ref[span, lanes])
-            delta = jnp.sum(probs * d_probs, axis=-1, keepdims=True)
-            ds = (probs * (d_probs - delta)).astype(BF)
-            res_ref[rows, lanes] = jnp.where(mine, nn(ds, k), res_ref[rows, lanes])
-            res_ref[span, k_lanes] += tn(ds, qm)
-            dv_ref[span, lanes] += tn(probs.astype(BF), dom)
+            q, do, k, v = q_ref[rows, lanes], d_att[rows, lanes], k_ref[span, lanes], v_ref[span, lanes]
+            products = do.astype(F32) * att[rows, lanes].astype(F32)
+            q_parts, do_parts, probs_parts, ds_parts, dq_parts = [], [], [], [], []
+            for h, mine in enumerate((first_head, jnp.logical_not(first_head))):
+                q_parts.append(jnp.where(mine, q, jnp.zeros_like(q)))
+                do_parts.append(jnp.where(mine, do, jnp.zeros_like(do)))
+                lse = jnp.sum(jnp.where(lane == 2 * j + h, lse_ref[rows, :], 0.0), axis=-1, keepdims=True)
+                delta = jnp.sum(jnp.where(mine, products, 0.0), axis=-1, keepdims=True)
+                probs = jnp.exp(nt(q_parts[h], k) + (bias_ref[:, :keys] - lse))
+                ds = (probs * (nt(do_parts[h], v) - delta)).astype(BF)
+                probs_parts.append(probs.astype(BF))
+                ds_parts.append(ds)
+                dq_parts.append(nn(ds, k))
+            res_ref[rows, lanes] = jnp.where(first_head, *dq_parts)
+            res_ref[span, k_lanes] += tn(jnp.concatenate(ds_parts), jnp.concatenate(q_parts))
+            dv_ref[span, lanes] += tn(jnp.concatenate(probs_parts), jnp.concatenate(do_parts))
             return carry
 
-        lax.fori_loop(first_head, last_head, head, 0)
-
-    heads = cols // HD
+        lax.fori_loop(first_pair, last_pair, pair, 0)
+
+    tiles = cols // LANES
     progress = {
         (0, 0): [("up", 0)],
         (1, 0): [("gate", 1)],
@@ -1043,7 +1046,7 @@
     for block in range(blocks):
         set_bias(block)
         for part in range(2):
-            attention_back(block, part * heads // 2, (part + 1) * heads // 2)
+            attention_back(block, *((0, tiles - 1), (tiles - 1, tiles))[part])
             for name, step in progress.get((block, part), ()):
                 advance(name, step)
 
@@ -1065,15 +1068,12 @@
     def qkv(name, source, lanes_at):
         row = chunks[name][0]
 
-        def piece_of(piece, carry):
-            lanes = pl.ds(pl.multiple_of(piece * LANES, LANES), LANES)
-            grad = tn(source[:, lanes_at : lanes_at + cols], normed1[:, lanes]).astype(BF)
-            for o in range(8):
-                at = pl.multiple_of(row + piece * low, 16)
-                pack[slot_of(o)[0], pl.ds(at, low), :] = grad[o * low : (o + 1) * low, :]
-            return carry
-
-        lax.fori_loop(0, pieces, piece_of, 0)
+        grad = tn(source[:, lanes_at : lanes_at + cols], normed1[...]).astype(BF)
+        for o in range(8):
+            slot = slot_of(o)[0]
+            for piece in range(pieces):
+                part = grad[o * low : (o + 1) * low, piece * LANES : (piece + 1) * LANES]
+                pack[slot, pl.ds(row + piece * low, low), :] = part
         start(name, 0)
 
     qkv("value", d_up, 0)
@@ -1109,7 +1109,7 @@
     turned_low = turned.astype(BF)
     rest = turned - turned_low.astype(F32)
     both = jnp.where(lane < LANES // 2, turned, pltpu.roll(rest, LANES // 2, 1)).astype(BF)
-    spread("gains", 0, both, 1)
+    spread("gains", 0, both)
     start("gains", 0)
     advance("value", 0)
 
@@ -1195,7 +1195,7 @@
         return pltpu.VMEM(dims, F32)
 
     scratch = [
-        low(length, width), low(length, width), pltpu.VMEM((1, length), jnp.int32), full(length, LANES),
+        low(length, width), low(length, width), pltpu.VMEM((1, length), jnp.int32),
         low(width, cols), low(width, cols), low(width, cols), low(width, width), low(width, ff), low(width, ff), low(ff, width),
         low(length, width), low(length, cols), low(length, cols), low(length, cols), low(length, cols), low(length, cols),
         full(length, LANES), full(TB, 3 * TB),

time: 147 us -> 140 us (0.952)
  Pallas kernels: 134 us -> 128 us
    pallas_call x1, Pallas kernels: 134 us -> 128 us  [fused_shards(): pl.pallas_call(block_kernel, out_shape=(shape(half_tokens, width), shape(...]
where the time goes in v3:
time: 140 us
  Pallas kernels  128 us (91%)
  local copies, waits for them, and re-layouts  9.41 us (7%)
  other arithmetic  2.25 us (2%)
    pallas_call x1, Pallas kernels, fused_shards(): pl.pallas_call(block_kernel, out_shape=(shape(half_tokens, width), shape(...  128 us

profile of v3, /device:TPU:0, one launch (start us, length us, event | category | flops | bytes accessed | tf_op | source)
XLA Modules:
  0.0 140.0 jit_solution(11473656488725790767)
XLA Ops:
  0.7 1.3 reshape.165.gain_one
  1.9 1.3 reshape.167.gain_two
  3.2 127.6 %block.1 = (bf16[512,768]{1,0:T(8,128)(2,1)}, bf16[512,768]{1,0:T(8,128)(2,1)}, f32[2,1488,128]{2,1,0:T(8,128)}) custom-call(bf16[512,768]{1,0:T(8,128)(2,1)} %bitcast.59, s32[1,512]{1,0:T(1,128)} %ids_hbm.1, bf16[512,768]{1,0:T(8,128)(2,1)} %bitcast.60, bf16[768,768]{1,0:T(8,128)(2,1)} %wq_hbm.1, bf16[768,768]{1,0:T(8,128)(2,1)} %wk_hbm.1, ...), custom_call_target="tpu_custom_call" | custom-call | tf_op jit(solution)/shard_map/block/pallas_call | solution.py:1210
  130.8 0.0 copy-start
  130.8 0.8 fusion.6
  131.6 0.7 fusion.1
  132.4 0.7 fusion.2
  133.1 0.8 fusion.5
  133.9 1.0 fusion.4
  134.9 0.7 copy_bitcast_fusion.2
  135.6 0.0 copy-done
  135.7 0.0 copy-start.2
  135.7 0.7 copy_bitcast_fusion.3
  136.4 0.1 copy.41
  136.6 0.1 copy.42
  136.7 0.0 copy-start.1
  136.7 0.8 copy_bitcast_fusion
  137.5 0.7 copy_bitcast_fusion.5
  138.2 0.0 copy-done.2
  138.2 0.9 copy.60
  139.1 0.0 copy-done.1
  139.1 0.9 copy.61
  (9 shorter events, 0.2 us)
Async XLA Ops:
  130.8 4.8 %copy-start = (f32[2,1488,128]{2,1,0:T(8,128)S(1)}, f32[2,1488,128]{2,1,0:T(8,128)}, u32[]{:S(2)}) copy-start(f32[2,1488,128]{2,1,0:T(8,128)} %get-tuple-element.16) | copy-start | bytes 4571140
  135.7 2.5 %copy-start.2 = (bf16[512,768]{1,0:T(8,128)(2,1)S(1)}, bf16[512,768]{1,0:T(8,128)(2,1)}, u32[]{:S(2)}) copy-start(bf16[512,768]{1,0:T(8,128)(2,1)} %get-tuple-element.14) | copy-start | bytes 2359300
  136.7 2.4 %copy-start.1 = (bf16[512,768]{1,0:T(8,128)(2,1)S(1)}, bf16[512,768]{1,0:T(8,128)(2,1)}, u32[]{:S(2)}) copy-start(bf16[512,768]{1,0:T(8,128)(2,1)} %get-tuple-element.15) | copy-start | bytes 2359300

commit v4 on v3

--- a/solution.py
+++ b/solution.py
@@ -598,6 +598,22 @@
 MESH = pl.DeviceIdType.MESH
 
 
+PLAN = {
+    "u0": (("down", 0),),
+    "a21": (("down", 1), ("gate", 0),),
+    "a30": (("out", 0),),
+    "a32": (("up", 0),),
+    "lower": (("gate", 1),),
+    "value": (("out", 1),),
+    "query": (("down", 2),),
+    "f1": (("up", 1),),
+    "f3": (("gate", 2), ("query", 0),),
+    "inp": (("down", 3),),
+    "end": (("up", 2), ("value", 0), ("key", 0), ("out", 2), ("gate", 3), ("gains", 0), ("query", 1), ("value", 1), ("key", 1), ("gains", 1), ("up", 3), ("query", 2), ("out", 3), ("value", 2), ("key", 2), ("gains", 2), ("query", 3), ("value", 3), ("key", 3), ("gains", 3),),
+}
+Z_FIRST = ("up", "value")
+
+
 def bit(value, place):
     return (value // (1 << place)) % 2
 
@@ -644,21 +660,26 @@
 
     bx, by, bz, bw = (bit(chip, i) for i in range(4))
     step_x, step_y = 1 - 2 * bx, 2 * (1 - 2 * by)
-    partners = (
-        chip + (1 - core) * step_x + core * step_y,
-        chip + core * step_x + (1 - core) * step_y,
-        chip + 4 * (1 - 2 * bz),
-        chip + 8 * (1 - 2 * bw),
-    )
+    near = chip + (1 - core) * step_x + core * step_y
+    aside = chip + core * step_x + (1 - core) * step_y
+    above = chip + 4 * (1 - 2 * bz)
+    across = chip + 8 * (1 - 2 * bw)
+    partners = (near, aside, above, across)
     holds = bw == core
 
-    def slot_of(owner):
+    def path_of(name):
+        return (above, near, aside, across) if name in Z_FIRST else partners
+
+    def slot_of(name, owner):
         kx, ky, kz = other_bit(bx, owner & 1), other_bit(by, (owner >> 1) & 1), other_bit(bz, (owner >> 2) & 1)
         first = (1 - core) * kx + core * ky
         second = core * kx + (1 - core) * ky
-        return first * 4 + second * 2 + kz, other_bit(bw, (owner >> 3) & 1)
-
-    def owner_of(first, second, third):
+        slot = kz * 4 + first * 2 + second if name in Z_FIRST else first * 4 + second * 2 + kz
+        return slot, other_bit(bw, (owner >> 3) & 1)
+
+    def owner_of(name, first, second, third):
+        if name in Z_FIRST:
+            first, second, third = second, third, first
         kx = (1 - core) * first + core * second
         ky = core * first + (1 - core) * second
         return other_bit(bx, kx) + 2 * other_bit(by, ky) + 4 * other_bit(bz, third)
@@ -739,7 +760,7 @@
             src, dst = pack.at[0, pl.ds(row + count // 2, count // 2)], got4.at[pl.ds(row, count // 2)]
         return pltpu.make_async_remote_copy(
             src_ref=src, dst_ref=dst, send_sem=hop_send.at[at], recv_sem=hop_recv.at[at],
-            device_id={"dp": partners[step], "seq": core}, device_id_type=MESH,
+            device_id={"dp": path_of(name)[step], "seq": core}, device_id_type=MESH,
         )
 
     def start(name, step):
@@ -793,6 +814,20 @@
                 for c in range(2):
                     rows = pl.ds(row + p * each + c * half, half)
                     final[c, pl.ds(at + p * half, half), :] = acc[rows, :] + got4[rows, :].astype(F32)
+
+    def proceed(point, here=None):
+        steps = PLAN.get(point, ())
+        if not steps:
+            return
+        if here is None:
+            for name, step in steps:
+                advance(name, step)
+            return
+
+        @pl.when(here)
+        def _():
+            for name, step in steps:
+                advance(name, step)
 
     def drain(name):
         for step in range(3):
@@ -884,10 +919,8 @@
     def feed(t, carry):
         rows = rows_of(t)
         local = rows_of(t % half_blocks)
-        is_own = t // half_blocks == core
         send_att(t).wait_recv()
         x = xs[rows, :].astype(F32)
-        dy = dys[rows, :]
         residual = x + (nn(att[rows, :], wo[own_cols, :]) + nn(att_other[rows, :], wo[other_cols, :]))
         res_ref[rows, :] = residual
         r = lax.rsqrt(jnp.mean(residual * residual, axis=-1, keepdims=True) + EPS)
@@ -895,31 +928,60 @@
         normed2[rows, :] = n2
         gate = nn(n2, wg[...])
         up = nn(n2, wu[...])
+        hidden[rows, :] = (gate * (1.0 / (1.0 + jnp.exp(-gate))) * up).astype(BF)
+        d_gate[rows, :] = gate.astype(BF)
+        d_up[rows, :] = up.astype(BF)
+        return carry
+
+    lax.fori_loop(0, blocks, feed, 0)
+
+    def spread(name, piece, grad):
+        row, rows = chunks[name][:2]
+        for o in range(16):
+            slot, far = slot_of(name, o)
+            at = pl.multiple_of(row + far * (rows // 2) + piece * low, 16)
+            pack[slot, pl.ds(at, low), :] = grad[o * low : (o + 1) * low, :]
+
+    def down_part(part, carry):
+        at = part * (ff // 2)
+        grad = tn(dys[...], hidden[:, pl.ds(pl.multiple_of(at, LANES), ff // 2)]).astype(BF)
+        for piece in range(ff // 2 // LANES):
+            spread("down", part * (ff // 2 // LANES) + piece, grad[:, piece * LANES : (piece + 1) * LANES])
+        return carry
+
+    lax.fori_loop(0, 2, down_part, 0)
+    start("down", 0)
+
+    def feed_back(t, carry):
+        rows = rows_of(t)
+        local = rows_of(t % half_blocks)
+        is_own = t // half_blocks == core
+        gate = d_gate[rows, :].astype(F32)
+        up = d_up[rows, :].astype(F32)
         sig = 1.0 / (1.0 + jnp.exp(-gate))
-        act = gate * sig
-        hid = (act * up).astype(BF)
-        hidden[rows, :] = hid
-        d_hidden = nt(dy, wd[...])
+        d_hidden = nt(dys[rows, :], wd[...])
         dg = (d_hidden * up * (sig * (1.0 + gate * (1.0 - sig)))).astype(BF)
-        du = (d_hidden * act).astype(BF)
+        du = (d_hidden * (gate * sig)).astype(BF)
         d_gate[rows, :] = dg
         d_up[rows, :] = du
         dn_own[rows, :] = (nt(dg, wg[...]) + nt(du, wu[...])).astype(BF)
         send_dn(t).start()
-        down = nn(hid, wd[...])
+        down = nn(hidden[rows, :], wd[...])
 
         @pl.when(is_own)
         def _():
-            out_keep[local, :] = residual + down
+            out_keep[local, :] = res_ref[rows, :] + down
 
         @pl.when(jnp.logical_not(is_own))
         def _():
             out_send[local, :] = down.astype(BF)
             send_out(t % half_blocks).start()
 
+        for n in range(blocks):
+            proceed(f"fb{n}", t == n)
         return carry
 
-    lax.fori_loop(0, blocks, feed, 0)
+    lax.fori_loop(0, blocks, feed_back, 0)
 
     wide = ff // 8
     pieces = width // LANES
@@ -929,7 +991,7 @@
 
         cuts = []
         for j in range(4):
-            owner = owner_of(first, j // 2, j % 2)
+            owner = owner_of(name, first, j // 2, j % 2)
             cuts.append(source[:, pl.ds(pl.multiple_of(owner * wide, wide), wide)])
         grad = tn(jnp.concatenate(cuts, axis=1), normed2[...]).astype(BF)
         for j in range(4):
@@ -939,28 +1001,14 @@
 
     gate_up("gate", d_gate, 1)
     start("gate", 0)
+    proceed("g1")
     gate_up("gate", d_gate, 0)
+    proceed("g0")
     gate_up("up", d_up, 1)
     start("up", 0)
+    proceed("u1")
     gate_up("up", d_up, 0)
-
-    def spread(name, piece, grad):
-        row, rows = chunks[name][:2]
-        for o in range(16):
-            slot, far = slot_of(o)
-            at = pl.multiple_of(row + far * (rows // 2) + piece * low, 16)
-            pack[slot, pl.ds(at, low), :] = grad[o * low : (o + 1) * low, :]
-
-    def down_part(part, carry):
-        at = part * (ff // 2)
-        grad = tn(dys[...], hidden[:, pl.ds(pl.multiple_of(at, LANES), ff // 2)]).astype(BF)
-        for piece in range(ff // 2 // LANES):
-            spread("down", part * (ff // 2 // LANES) + piece, grad[:, piece * LANES : (piece + 1) * LANES])
-        return carry
-
-    lax.fori_loop(0, 2, down_part, 0)
-    start("down", 0)
-    advance("gate", 0)
+    proceed("u0")
 
 
     d_branch, d_att = normed2, hidden
@@ -990,6 +1038,8 @@
             write_out(t % half_blocks).start()
             out_keep[local, :] = grad
 
+        for n in range(blocks):
+            proceed(f"n{n}", t == n)
         return carry
 
     lax.fori_loop(0, blocks, norm_two, 0)
@@ -999,11 +1049,12 @@
     for piece in range(cols // LANES):
         spread("out", piece, out_grad[:, piece * LANES : (piece + 1) * LANES])
     start("out", 0)
+    proceed("out")
 
     res_ref[:, cols:] = jnp.zeros((length, cols), F32)
     dv_ref[...] = jnp.zeros_like(dv_ref)
 
-    def attention_back(block, first_pair, last_pair):
+    def attention_back(block):
         first = window(block)
         keys = (block + 1) * TB - first
         rows = pl.ds(block * TB, TB)
@@ -1029,26 +1080,15 @@
             res_ref[rows, lanes] = jnp.where(first_head, *dq_parts)
             res_ref[span, k_lanes] += tn(jnp.concatenate(ds_parts), jnp.concatenate(q_parts))
             dv_ref[span, lanes] += tn(jnp.concatenate(probs_parts), jnp.concatenate(do_parts))
+            for n in range(cols // LANES):
+                proceed(f"a{block}{n}", j == n)
             return carry
 
-        lax.fori_loop(first_pair, last_pair, pair, 0)
-
-    tiles = cols // LANES
-    progress = {
-        (0, 0): [("up", 0)],
-        (1, 0): [("gate", 1)],
-        (1, 1): [("down", 0)],
-        (2, 0): [("up", 1), ("gate", 2)],
-        (2, 1): [("out", 0), ("down", 1)],
-        (3, 0): [("up", 2), ("out", 1)],
-        (3, 1): [("down", 2), ("gate", 3)],
-    }
+        lax.fori_loop(0, cols // LANES, pair, 0)
+
     for block in range(blocks):
         set_bias(block)
-        for part in range(2):
-            attention_back(block, *((0, tiles - 1), (tiles - 1, tiles))[part])
-            for name, step in progress.get((block, part), ()):
-                advance(name, step)
+        attention_back(block)
 
     def lower(t, carry):
         rows = rows_of(t)
@@ -1064,23 +1104,23 @@
         return carry
 
     lax.fori_loop(0, blocks, lower, 0)
+    proceed("lower")
 
     def qkv(name, source, lanes_at):
         row = chunks[name][0]
 
         grad = tn(source[:, lanes_at : lanes_at + cols], normed1[...]).astype(BF)
         for o in range(8):
-            slot = slot_of(o)[0]
+            slot = slot_of(name, o)[0]
             for piece in range(pieces):
                 part = grad[o * low : (o + 1) * low, piece * LANES : (piece + 1) * LANES]
                 pack[slot, pl.ds(row + piece * low, low), :] = part
         start(name, 0)
+        proceed(name)
 
     qkv("value", d_up, 0)
     qkv("query", d_gate, 0)
     qkv("key", d_gate, cols)
-    advance("up", 3)
-    advance("out", 2)
 
     def finish(j, carry):
         t = ((1 - core) * half_blocks + j) % blocks
@@ -1102,6 +1142,8 @@
             out_send[local, :] = dn.astype(BF)
             send_dn1(t % half_blocks).start()
 
+        for n in range(blocks):
+            proceed(f"f{n}", j == n)
         return carry
 
     lax.fori_loop(0, blocks, finish, 0)
@@ -1111,7 +1153,7 @@
     both = jnp.where(lane < LANES // 2, turned, pltpu.roll(rest, LANES // 2, 1)).astype(BF)
     spread("gains", 0, both)
     start("gains", 0)
-    advance("value", 0)
+    proceed("gains")
 
     def input_part(t, carry):
         local = rows_of(t)
@@ -1126,25 +1168,15 @@
         return carry
 
     lax.fori_loop(0, half_blocks, input_part, 0)
-    advance("query", 0)
-    advance("value", 1)
-    advance("down", 3)
-    advance("out", 3)
+    proceed("inp")
     early = chunks["query"][5]
+    steps = PLAN["end"]
+    last = max([i + 1 for i, (name, step) in enumerate(steps) if step == 3 and chunks[name][5] < early], default=0)
+    for name, step in steps[:last]:
+        advance(name, step)
     send_final(0, 0, early).start()
-    advance("key", 0)
-    advance("query", 1)
-    advance("value", 2)
-    advance("gains", 0)
-    advance("key", 1)
-    advance("query", 2)
-    advance("gains", 1)
-    advance("key", 2)
-    advance("gains", 2)
-    advance("value", 3)
-    advance("query", 3)
-    advance("key", 3)
-    advance("gains", 3)
+    for name, step in steps[last:]:
+        advance(name, step)
     rows_final = final.shape[1]
     send_final(1, early, rows_final - early).start()
     mine_out = load(0, final.at[core], final_out.at[0])

time: 140 us -> 116 us (0.83)
  Pallas kernels: 128 us -> 104 us
    pallas_call x1, Pallas kernels: 128 us -> 104 us  [fused_shards(): pl.pallas_call(block_kernel, out_shape=(shape(half_tokens, width), shape(...]
where the time goes in v4:
time: 116 us
  Pallas kernels  104 us (90%)
  local copies, waits for them, and re-layouts  9.41 us (8%)
  other arithmetic  2.25 us (2%)
    pallas_call x1, Pallas kernels, fused_shards(): pl.pallas_call(block_kernel, out_shape=(shape(half_tokens, width), shape(...  104 us

profile of v4, /device:TPU:0, one launch (start us, length us, event | category | flops | bytes accessed | tf_op | source)
XLA Modules:
  0.0 115.9 jit_solution(8188749386268418716)
XLA Ops:
  0.7 1.3 %reshape.165.gain_one = f32[1,768]{1,0:T(1,128)} reshape(bf16[768]{0:T(1024)(128)(2,1)} %param.18) | data formatting | bytes 4608 | tf_op jit(solution)/shard_map/reshape | solution.py:1255
  1.9 1.3 %reshape.167.gain_two = f32[1,768]{1,0:T(1,128)} reshape(bf16[768]{0:T(1024)(128)(2,1)} %param.23) | data formatting | bytes 4608 | tf_op jit(solution)/shard_map/reshape | solution.py:1255
  3.2 103.5 %block.1 = (bf16[512,768]{1,0:T(8,128)(2,1)}, bf16[512,768]{1,0:T(8,128)(2,1)}, f32[2,1488,128]{2,1,0:T(8,128)}) custom-call(bf16[512,768]{1,0:T(8,128)(2,1)} %bitcast.59, s32[1,512]{1,0:T(1,128)} %ids_hbm.1, bf16[512,768]{1,0:T(8,128)(2,1)} %bitcast.60, bf16[768,768]{1,0:T(8,128)(2,1)} %wq_hbm.1, bf16[768,768]{1,0:T(8,128)(2,1)} %wk_hbm.1, ...), custom_call_target="tpu_custom_call" | custom-call | tf_op jit(solution)/shard_map/block/pallas_call | solution.py:1242
  106.7 0.0 copy-start
  106.7 0.8 fusion.6
  107.5 0.7 fusion.1
  108.3 0.7 fusion.2
  109.0 0.8 fusion.5
  109.9 1.0 fusion.4
  110.8 0.7 copy_bitcast_fusion.2
  111.5 0.0 copy-done
  111.6 0.0 copy-start.2
  111.7 0.7 copy_bitcast_fusion.3
  112.4 0.1 copy.41
  112.5 0.1 copy.42
  112.6 0.0 copy-start.1
  112.6 0.8 copy_bitcast_fusion
  113.5 0.7 copy_bitcast_fusion.5
  114.2 0.0 copy-done.2
  114.2 0.9 copy.60
  115.0 0.0 copy-done.1
  115.0 0.9 copy.61
  (9 shorter events, 0.2 us)
Async XLA Ops:
  106.7 4.8 %copy-start = (f32[2,1488,128]{2,1,0:T(8,128)S(1)}, f32[2,1488,128]{2,1,0:T(8,128)}, u32[]{:S(2)}) copy-start(f32[2,1488,128]{2,1,0:T(8,128)} %get-tuple-element.16) | copy-start | bytes 4571140
  111.6 2.5 %copy-start.2 = (bf16[512,768]{1,0:T(8,128)(2,1)S(1)}, bf16[512,768]{1,0:T(8,128)(2,1)}, u32[]{:S(2)}) copy-start(bf16[512,768]{1,0:T(8,128)(2,1)} %get-tuple-element.14) | copy-start | bytes 2359300
  112.6 2.4 %copy-start.1 = (bf16[512,768]{1,0:T(8,128)(2,1)S(1)}, bf16[512,768]{1,0:T(8,128)(2,1)}, u32[]{:S(2)}) copy-start(bf16[512,768]{1,0:T(8,128)(2,1)} %get-tuple-element.15) | copy-start | bytes 2359300

commit v5 on v4

--- a/solution.py
+++ b/solution.py
@@ -599,19 +599,17 @@
 
 
 PLAN = {
-    "u0": (("down", 0),),
-    "a21": (("down", 1), ("gate", 0),),
-    "a30": (("out", 0),),
-    "a32": (("up", 0),),
-    "lower": (("gate", 1),),
-    "value": (("out", 1),),
-    "query": (("down", 2),),
-    "f1": (("up", 1),),
-    "f3": (("gate", 2), ("query", 0),),
-    "inp": (("down", 3),),
-    "end": (("up", 2), ("value", 0), ("key", 0), ("out", 2), ("gate", 3), ("gains", 0), ("query", 1), ("value", 1), ("key", 1), ("gains", 1), ("up", 3), ("query", 2), ("out", 3), ("value", 2), ("key", 2), ("gains", 2), ("query", 3), ("value", 3), ("key", 3), ("gains", 3),),
+    "n0": (("down", 0),),
+    "a22": (("down", 1),),
+    "a30": (("up", 0),),
+    "a31": (("gate", 0), ("out", 0),),
+    "lower": (("down", 2),),
+    "d1": (("up", 1),),
+    "f1": (("down", 3), ("gate", 1), ("out", 1),),
+    "f3": (("value", 0), ("query", 0),),
+    "end": (("up", 2), ("gate", 2), ("out", 2), ("key", 0), ("query", 1), ("value", 1), ("gains", 0), ("key", 1), ("up", 3), ("value", 2), ("query", 2), ("gains", 1), ("gate", 3), ("key", 2), ("out", 3), ("gains", 2), ("value", 3), ("query", 3), ("key", 3), ("gains", 3),),
 }
-Z_FIRST = ("up", "value")
+Z_FIRST = ("gate", "value",)
 
 
 def bit(value, place):
@@ -637,11 +635,11 @@
 
 
 def block_kernel(
-    x_hbm, ids_hbm, dy_hbm, wq_hbm, wk_hbm, wv_hbm, wo_hbm, wg_hbm, wu_hbm, wd_hbm, gain_one, gain_two,
+    x_hbm, ids_hbm, dy_hbm, wq_hbm, wk_hbm, wv_hbm, wo_hbm, wg_hbm, wu_hbm, wd_hbm, gain_one_low, gain_two_low,
     cos_f, sin_f, cos_c, sin_c,
     block_out, input_grad, final_out,
     xs, dys, ids, wq, wk, wv, wo, wg, wu, wd, normed1, q_ref, k_ref, v_ref, att, att_other, lse_ref, bias_ref,
-    res_ref, normed2, hidden, d_gate, d_up, dn_own, dn_other, out_keep, out_send, out_got, dv_ref, dn_keep, dn_got,
+    gain_one, gain_two, res_ref, normed2, hidden, d_gate, d_up, dn_own, dn_other, d_res, out_send, out_got, dv_ref, dn_keep, dn_got,
     gains, pack, got1, got2, got3, got4, acc, final, final_got,
     load_sem, pair_send, pair_recv, hop_send, hop_recv,
 ):
@@ -708,7 +706,7 @@
         load(8, wd_hbm.at[own_ff, :], wd),
         load(9, dy_hbm, dys.at[own_rows]),
     ]
-    for copy in loads:
+    for copy in loads[:5]:
         copy.start()
 
     def to_pair(i, src, dst):
@@ -836,12 +834,16 @@
             hop(name, 3).wait_send()
 
 
+    gain_one[...] = gain_one_low[...].astype(F32).reshape(1, width)
+    gain_two[...] = gain_two_low[...].astype(F32).reshape(1, width)
     pl.semaphore_wait(barrier, len(everyone))
     send_x.start()
     send_ids.start()
-    send_dy.start()
     for copy in loads[:4]:
         copy.wait()
+    for copy in loads[5:]:
+        copy.start()
+    send_dy.start()
 
     def project(j, carry):
         t = (core * half_blocks + j) % blocks
@@ -923,6 +925,11 @@
         x = xs[rows, :].astype(F32)
         residual = x + (nn(att[rows, :], wo[own_cols, :]) + nn(att_other[rows, :], wo[other_cols, :]))
         res_ref[rows, :] = residual
+
+        @pl.when(t // half_blocks == core)
+        def _():
+            dn_keep[local, :] = residual
+
         r = lax.rsqrt(jnp.mean(residual * residual, axis=-1, keepdims=True) + EPS)
         n2 = (residual * r * gain_two[...]).astype(BF)
         normed2[rows, :] = n2
@@ -954,8 +961,6 @@
 
     def feed_back(t, carry):
         rows = rows_of(t)
-        local = rows_of(t % half_blocks)
-        is_own = t // half_blocks == core
         gate = d_gate[rows, :].astype(F32)
         up = d_up[rows, :].astype(F32)
         sig = 1.0 / (1.0 + jnp.exp(-gate))
@@ -966,17 +971,6 @@
         d_up[rows, :] = du
         dn_own[rows, :] = (nt(dg, wg[...]) + nt(du, wu[...])).astype(BF)
         send_dn(t).start()
-        down = nn(hidden[rows, :], wd[...])
-
-        @pl.when(is_own)
-        def _():
-            out_keep[local, :] = res_ref[rows, :] + down
-
-        @pl.when(jnp.logical_not(is_own))
-        def _():
-            out_send[local, :] = down.astype(BF)
-            send_out(t % half_blocks).start()
-
         for n in range(blocks):
             proceed(f"fb{n}", t == n)
         return carry
@@ -1011,7 +1005,7 @@
     proceed("u0")
 
 
-    d_branch, d_att = normed2, hidden
+    d_branch, d_att = normed2, att_other
     gains[...] = jnp.zeros_like(gains)
 
     def norm_two(t, carry):
@@ -1028,22 +1022,18 @@
         grad = dy + r * (e - scaled * (r * jnp.mean(e * residual, axis=-1, keepdims=True)))
         small = grad.astype(BF)
         d_branch[rows, :] = small
-        d_att[rows, 0:cols] = nt(small, wo[own_cols, :]).astype(BF)
+        d_att[rows, :] = nt(small, wo[own_cols, :]).astype(BF)
 
         @pl.when(is_own)
         def _():
             gains[0:1, :] += jnp.sum(dn * scaled, axis=0, keepdims=True)
-            send_out(t % half_blocks).wait_recv()
-            out_got[local, :] = (out_keep[local, :] + out_got[local, :].astype(F32)).astype(BF)
-            write_out(t % half_blocks).start()
-            out_keep[local, :] = grad
+            d_res[local, :] = grad
 
         for n in range(blocks):
             proceed(f"n{n}", t == n)
         return carry
 
     lax.fori_loop(0, blocks, norm_two, 0)
-    d_res = out_keep
 
     out_grad = tn(d_branch[...], att[...]).astype(BF)
     for piece in range(cols // LANES):
@@ -1121,6 +1111,35 @@
     qkv("value", d_up, 0)
     qkv("query", d_gate, 0)
     qkv("key", d_gate, cols)
+
+    def down_product(j, carry):
+        t = ((1 - core) * half_blocks + j) % blocks
+        local = rows_of(t % half_blocks)
+        down = nn(hidden[rows_of(t), :], wd[...])
+
+        @pl.when(j < half_blocks)
+        def _():
+            out_send[local, :] = down.astype(BF)
+            send_out(t % half_blocks).start()
+
+        @pl.when(j >= half_blocks)
+        def _():
+            dn_keep[local, :] += down
+
+        for n in range(blocks):
+            proceed(f"d{n}", j == n)
+        return carry
+
+    lax.fori_loop(0, blocks, down_product, 0)
+
+    def write_block(t, carry):
+        local = rows_of(t)
+        send_out(t).wait_recv()
+        out_got[local, :] = (dn_keep[local, :] + out_got[local, :].astype(F32)).astype(BF)
+        write_out(t).start()
+        return carry
+
+    lax.fori_loop(0, half_blocks, write_block, 0)
 
     def finish(j, carry):
         t = ((1 - core) * half_blocks + j) % blocks
@@ -1206,6 +1225,35 @@
     late_out.wait()
 
 
+def hand_out(
+    final, block_out, input_grad,
+    block_out_ref, input_grad_ref, gain_one, query, key, value, out, gain_two, gate, up, down,
+):
+    core = lax.axis_index("seq")
+    taken = other_bit(bit(lax.axis_index("dp"), 3), core)
+    width = block_out.shape[1]
+    chunks, _, _ = layout_of(width, width // 2, down.shape[1] // 2)
+    block_out_ref[...] = block_out[...]
+    input_grad_ref[...] = input_grad[...]
+    targets = {"query": query, "key": key, "value": value, "out": out, "gate": gate, "up": up, "down": down}
+    for name, target in targets.items():
+        _, _, kind, pieces, each, at = chunks[name]
+        half = each // 2
+        for p in range(pieces):
+            rows = pl.ds(at + p * half, half)
+            if kind == "B":
+                target[:, p * LANES : (p + 1) * LANES] = final[taken, rows, :]
+            else:
+                for whose in range(2):
+                    first = ((core if whose == 0 else 1 - core) * pieces + p) * LANES
+                    target[:, pl.ds(pl.multiple_of(first, LANES), LANES)] = final[whose, rows, :]
+    _, _, _, _, each, at = chunks["gains"]
+    rows = pl.ds(at, each // 2)
+    both = jnp.transpose(final[0, rows, :] + final[1, rows, :])
+    gain_two[...] = (both[0:1] + both[LANES // 2 : LANES // 2 + 1]).reshape(each // 2)
+    gain_one[...] = (both[1:2] + both[LANES // 2 + 1 : LANES // 2 + 2]).reshape(each // 2)
+
+
 def fused_shards(
     tokens, segment_ids, norm1_gain, w_query, w_key, w_value, w_out, norm2_gain, w_gate, w_up, w_down, out_grad,
 ):
@@ -1230,7 +1278,7 @@
         low(length, width), low(length, width), pltpu.VMEM((1, length), jnp.int32),
         low(width, cols), low(width, cols), low(width, cols), low(width, width), low(width, ff), low(width, ff), low(ff, width),
         low(length, width), low(length, cols), low(length, cols), low(length, cols), low(length, cols), low(length, cols),
-        full(length, LANES), full(TB, 3 * TB),
+        full(length, LANES), full(TB, 3 * TB), full(1, width), full(1, width),
         full(length, width), low(length, width), low(length, ff), low(length, ff), low(length, ff), low(length, width),
         low(length, width), full(half_tokens, width), low(half_tokens, width), low(half_tokens, width), full(length, cols),
         full(half_tokens, width), low(half_tokens, width),
@@ -1252,35 +1300,24 @@
     )(
         tokens.reshape(half_tokens, width), segment_ids.reshape(1, half_tokens), out_grad.reshape(half_tokens, width),
         w_query, w_key, w_value, w_out, w_gate, w_up, w_down,
-        norm1_gain.astype(F32).reshape(1, width), norm2_gain.astype(F32).reshape(1, width), *tables,
+        norm1_gain, norm2_gain, *tables,
     )
-    mine, got = final[0], final[1]
-    holds = (chip >> 3) == core
-
-    def part(name):
-        _, _, kind, pieces, each, at = chunks[name]
-        half = each // 2
-        cut = slice(at, at + pieces * half)
-        a, b = mine[cut].reshape(pieces, half, LANES), got[cut].reshape(pieces, half, LANES)
-        if kind == "B":
-            taken = jnp.where(holds, a, b)
-        else:
-            taken = jnp.where(core == 0, jnp.concatenate([a, b]), jnp.concatenate([b, a]))
-        return jnp.transpose(taken, (0, 2, 1)).reshape(-1, half)
-
-    gains = part("gains")
-    gains = gains[:LANES] + gains[LANES:]
-    summed = (
-        gains[1] + gains[1 + LANES // 2],
-        part("query"),
-        part("key"),
-        part("value"),
-        part("out"),
-        gains[0] + gains[LANES // 2],
-        part("gate"),
-        part("up"),
-        part("down"),
-    )
+    columns, columns_ff = width // 32, ff // 16
+    outs = [shape(half_tokens, width), shape(half_tokens, width)] + [
+        shape(*dims, dtype=F32)
+        for dims in (
+            (columns,), (columns, width), (columns, width), (columns, width), (columns, width), (columns,),
+            (columns_ff, width), (columns_ff, width), (columns, 2 * ff),
+        )
+    ]
+    block_out, input_grad, *summed = pl.pallas_call(
+        hand_out,
+        out_shape=outs,
+        in_specs=[vmem] * 3,
+        out_specs=[vmem] * len(outs),
+        name="hand_out",
+    )(final, block_out, input_grad)
+    summed = [a.T if a.ndim == 2 else a for a in summed]
     return (block_out.reshape(seqs, half_tokens, width), input_grad.reshape(seqs, half_tokens, width), *summed)
 
 

time: 116 us -> 106 us (0.914)
  local copies, waits for them, and re-layouts: 9.41 us -> 0 us
  other arithmetic: 2.25 us -> 0 us
    reshape x7 -> x0, local copies, waits for them, and re-layouts: 4.74 us -> none  [the longest x3 2.19 us: part(): return jnp.transpose(taken, (0, 2, 1)).reshape(-1, half)]
    pallas_call x0 -> x1, Pallas kernels: none -> 3.32 us  [fused_shards(): pl.pallas_call(hand_out, out_shape=outs, in_specs=[vmem] * 3, out_specs=[...]
    slice x3 -> x0, local copies, waits for them, and re-layouts: 2.59 us -> none  [the longest x2 1.75 us: part(): mine[cut].reshape(pieces, half, LANES)]
    pallas_call x1, Pallas kernels: 104 us -> 102 us  [fused_shards(): pl.pallas_call(block_kernel, out_shape=(shape(half_tokens, width), shape(...]
    unnamed x8 -> x0, local copies, waits for them, and re-layouts: 1.77 us -> none
where the time goes in v5:
time: 106 us
  Pallas kernels  105 us (99%)
    pallas_call x1, Pallas kernels, fused_shards(): pl.pallas_call(block_kernel, out_shape=(shape(half_tokens, width), shape(...  102 us
    pallas_call x1, Pallas kernels, fused_shards(): pl.pallas_call(hand_out, out_shape=outs, in_specs=[vmem] * 3, out_specs=[...  3.32 us

profile of v5, /device:TPU:0, one launch (start us, length us, event | category | flops | bytes accessed | tf_op | source)
XLA Modules:
  0.0 105.6 jit_solution(4917117096327992352)
XLA Ops:
  0.6 101.6 %block.1 = (bf16[512,768]{1,0:T(8,128)(2,1)}, bf16[512,768]{1,0:T(8,128)(2,1)}, f32[2,1488,128]{2,1,0:T(8,128)}) custom-call(bf16[512,768]{1,0:T(8,128)(2,1)} %bitcast.11, s32[1,512]{1,0:T(1,128)} %ids_hbm.1, bf16[512,768]{1,0:T(8,128)(2,1)} %bitcast.12, bf16[768,768]{1,0:T(8,128)(2,1)} %wq_hbm.1, bf16[768,768]{1,0:T(8,128)(2,1)} %wk_hbm.1, ...), custom_call_target="tpu_custom_call" | custom-call | tf_op jit(solution)/shard_map/block/pallas_call | solution.py:1290
  102.3 3.3 %hand_out.1 = (bf16[512,768]{1,0:T(8,128)(2,1)}, bf16[512,768]{1,0:T(8,128)(2,1)}, f32[24]{0:T(128)}, f32[24,768]{1,0:T(8,128)}, f32[24,768]{1,0:T(8,128)}, /*in...) custom-call(f32[2,1488,128]{2,1,0:T(8,128)} %get-tuple-element.25.fi, ...), custom_call_target="tpu_custom_call" | custom-call | tf_op jit(solution)/shard_map/hand_out/pallas_call | solution.py:1313

commit v6 on v5

--- a/solution.py
+++ b/solution.py
@@ -599,17 +599,24 @@
 
 
 PLAN = {
-    "n0": (("down", 0),),
-    "a22": (("down", 1),),
-    "a30": (("up", 0),),
-    "a31": (("gate", 0), ("out", 0),),
-    "lower": (("down", 2),),
-    "d1": (("up", 1),),
-    "f1": (("down", 3), ("gate", 1), ("out", 1),),
-    "f3": (("value", 0), ("query", 0),),
-    "end": (("up", 2), ("gate", 2), ("out", 2), ("key", 0), ("query", 1), ("value", 1), ("gains", 0), ("key", 1), ("up", 3), ("value", 2), ("query", 2), ("gains", 1), ("gate", 3), ("key", 2), ("out", 3), ("gains", 2), ("value", 3), ("query", 3), ("key", 3), ("gains", 3),),
+    "u0": (("down", 0),),
+    "a01": (("gate0", 0),),
+    "a10": (("up0", 0),),
+    "a20": (("down", 1),),
+    "a30": (("up0", 1), ("gate1", 0), ("up1", 0),),
+    "lower": (("down", 2), ("out", 0),),
+    "query": (("up0", 2),),
+    "key": (("up1", 1), ("gate0", 1),),
+    "f1": (("out", 1),),
+    "f2": (("down", 3),),
+    "f3": (("gate0", 2), ("gate1", 1),),
+    "gains": (("up0", 3),),
+    "d1": (("value", 0),),
+    "d2": (("query", 0),),
+    "inp": (("gate0", 3), ("up1", 2), ("gate1", 2), ("out", 2),),
+    "end": (("gains", 0), ("key", 0), ("query", 1), ("up1", 3), ("value", 1), ("gains", 1), ("gate1", 3), ("key", 1), ("query", 2), ("value", 2), ("out", 3), ("gains", 2), ("key", 2), ("query", 3), ("value", 3), ("gains", 3), ("key", 3),),
 }
-Z_FIRST = ("gate", "value",)
+Z_FIRST = ("gate0", "gate1", "value", "gains",)
 
 
 def bit(value, place):
@@ -624,7 +631,8 @@
     low, wide = width // 16, ff // 8
     table, row, final = {}, 0, 0
     for name, kind, pieces, each in (
-        ("gate", "B", width // LANES, wide), ("up", "B", width // LANES, wide), ("down", "A", ff // LANES, low),
+        ("gate0", "B", width // LANES // 2, wide), ("gate1", "B", width // LANES // 2, wide),
+        ("up0", "B", width // LANES // 2, wide), ("up1", "B", width // LANES // 2, wide), ("down", "A", ff // LANES, low),
         ("out", "A", cols // LANES, low), ("query", "B", width // LANES, low), ("key", "B", width // LANES, low),
         ("value", "B", width // LANES, low), ("gains", "A", 1, low),
     ):
@@ -846,13 +854,13 @@
     send_dy.start()
 
     def project(j, carry):
-        t = (core * half_blocks + j) % blocks
-
-        @pl.when(j == half_blocks)
+        t = (core + j) % 2
+
+        @pl.when(j == 1)
         def _():
             send_x.wait_recv()
 
-        rows = rows_of(t)
+        rows = pl.ds(pl.multiple_of(t * half_tokens, half_tokens), half_tokens)
         x = xs[rows, :].astype(F32)
         r = lax.rsqrt(jnp.mean(x * x, axis=-1, keepdims=True) + EPS)
         normed = (x * r * gain_one[...]).astype(BF)
@@ -860,9 +868,9 @@
         v_ref[rows, :] = nn(normed, wv[...]).astype(BF)
         q = nn(normed, wq[...]).astype(BF).astype(F32)
         k = nn(normed, wk[...]).astype(BF).astype(F32)
-        for sub in range(TB // 64):
-            cosine, sine, low_half = angle_block(tables, t * (TB // 64) + sub)
-            at = pl.ds(pl.multiple_of(t * TB + sub * 64, 64), 64)
+        for sub in range(half_tokens // 64):
+            cosine, sine, low_half = angle_block(tables, t * (half_tokens // 64) + sub)
+            at = pl.ds(pl.multiple_of(t * half_tokens + sub * 64, 64), 64)
             for tile in range(cols // LANES):
                 lanes = slice(tile * LANES, (tile + 1) * LANES)
                 part = slice(sub * 64, (sub + 1) * 64)
@@ -870,7 +878,7 @@
                 k_ref[at, lanes] = rotate(k[part, lanes], cosine, sine, low_half).astype(BF)
         return carry
 
-    lax.fori_loop(0, blocks, project, 0)
+    lax.fori_loop(0, 2, project, 0)
     loads[4].wait()
     send_ids.wait_recv()
     lse_ref[...] = jnp.transpose(jnp.broadcast_to(ids[...].astype(F32), (LANES, length)))
@@ -919,16 +927,16 @@
     other_cols = pl.ds(pl.multiple_of((1 - core) * cols, cols), cols)
 
     def feed(t, carry):
-        rows = rows_of(t)
-        local = rows_of(t % half_blocks)
-        send_att(t).wait_recv()
+        rows = pl.ds(pl.multiple_of(t * half_tokens, half_tokens), half_tokens)
+        for n in range(half_blocks):
+            send_att(t * half_blocks + n).wait_recv()
         x = xs[rows, :].astype(F32)
         residual = x + (nn(att[rows, :], wo[own_cols, :]) + nn(att_other[rows, :], wo[other_cols, :]))
         res_ref[rows, :] = residual
 
-        @pl.when(t // half_blocks == core)
+        @pl.when(t == core)
         def _():
-            dn_keep[local, :] = residual
+            dn_keep[...] = residual
 
         r = lax.rsqrt(jnp.mean(residual * residual, axis=-1, keepdims=True) + EPS)
         n2 = (residual * r * gain_two[...]).astype(BF)
@@ -940,7 +948,7 @@
         d_up[rows, :] = up.astype(BF)
         return carry
 
-    lax.fori_loop(0, blocks, feed, 0)
+    lax.fori_loop(0, 2, feed, 0)
 
     def spread(name, piece, grad):
         row, rows = chunks[name][:2]
@@ -981,25 +989,26 @@
     pieces = width // LANES
 
     def gate_up(name, source, first):
-        row = chunks[name][0]
-
         cuts = []
         for j in range(4):
-            owner = owner_of(name, first, j // 2, j % 2)
+            owner = owner_of(name + "0", first, j // 2, j % 2)
             cuts.append(source[:, pl.ds(pl.multiple_of(owner * wide, wide), wide)])
         grad = tn(jnp.concatenate(cuts, axis=1), normed2[...]).astype(BF)
         for j in range(4):
             for piece in range(pieces):
                 part = grad[j * wide : (j + 1) * wide, piece * LANES : (piece + 1) * LANES]
-                pack[4 * first + j, pl.ds(row + piece * wide, wide), :] = part
+                row = chunks[f"{name}{piece // (pieces // 2)}"][0] + piece % (pieces // 2) * wide
+                pack[4 * first + j, pl.ds(row, wide), :] = part
 
     gate_up("gate", d_gate, 1)
-    start("gate", 0)
+    start("gate0", 0)
+    start("gate1", 0)
     proceed("g1")
     gate_up("gate", d_gate, 0)
     proceed("g0")
     gate_up("up", d_up, 1)
-    start("up", 0)
+    start("up0", 0)
+    start("up1", 0)
     proceed("u1")
     gate_up("up", d_up, 0)
     proceed("u0")
@@ -1112,35 +1121,6 @@
     qkv("query", d_gate, 0)
     qkv("key", d_gate, cols)
 
-    def down_product(j, carry):
-        t = ((1 - core) * half_blocks + j) % blocks
-        local = rows_of(t % half_blocks)
-        down = nn(hidden[rows_of(t), :], wd[...])
-
-        @pl.when(j < half_blocks)
-        def _():
-            out_send[local, :] = down.astype(BF)
-            send_out(t % half_blocks).start()
-
-        @pl.when(j >= half_blocks)
-        def _():
-            dn_keep[local, :] += down
-
-        for n in range(blocks):
-            proceed(f"d{n}", j == n)
-        return carry
-
-    lax.fori_loop(0, blocks, down_product, 0)
-
-    def write_block(t, carry):
-        local = rows_of(t)
-        send_out(t).wait_recv()
-        out_got[local, :] = (dn_keep[local, :] + out_got[local, :].astype(F32)).astype(BF)
-        write_out(t).start()
-        return carry
-
-    lax.fori_loop(0, half_blocks, write_block, 0)
-
     def finish(j, carry):
         t = ((1 - core) * half_blocks + j) % blocks
         rows = rows_of(t)
@@ -1153,11 +1133,10 @@
 
         @pl.when(is_own)
         def _():
-            dn_keep[local, :] = dn
+            res_ref[rows, :] = dn
 
         @pl.when(jnp.logical_not(is_own))
         def _():
-            send_out(t % half_blocks).wait_send()
             out_send[local, :] = dn.astype(BF)
             send_dn1(t % half_blocks).start()
 
@@ -1174,10 +1153,31 @@
     start("gains", 0)
     proceed("gains")
 
+    def down_product(j, carry):
+        t = ((1 - core) * half_blocks + j) % blocks
+        local = rows_of(t % half_blocks)
+        down = nn(hidden[rows_of(t), :], wd[...])
+
+        @pl.when(j < half_blocks)
+        def _():
+            send_dn1(t % half_blocks).wait_send()
+            out_send[local, :] = down.astype(BF)
+            send_out(t % half_blocks).start()
+
+        @pl.when(j >= half_blocks)
+        def _():
+            dn_keep[local, :] += down
+
+        for n in range(blocks):
+            proceed(f"d{n}", j == n)
+        return carry
+
+    lax.fori_loop(0, blocks, down_product, 0)
+
     def input_part(t, carry):
         local = rows_of(t)
         send_dn1(t).wait_recv()
-        dn = dn_keep[local, :] + dn_got[local, :].astype(F32)
+        dn = res_ref[rows_of(core * half_blocks + t), :] + dn_got[local, :].astype(F32)
         x = xs[rows_of(core * half_blocks + t), :].astype(F32)
         r = lax.rsqrt(jnp.mean(x * x, axis=-1, keepdims=True) + EPS)
         e = gain_one[...] * dn
@@ -1187,6 +1187,15 @@
         return carry
 
     lax.fori_loop(0, half_blocks, input_part, 0)
+    def write_block(t, carry):
+        local = rows_of(t)
+        send_out(t).wait_recv()
+        out_got[local, :] = (dn_keep[local, :] + out_got[local, :].astype(F32)).astype(BF)
+        write_out(t).start()
+        return carry
+
+    lax.fori_loop(0, half_blocks, write_block, 0)
+
     proceed("inp")
     early = chunks["query"][5]
     steps = PLAN["end"]
@@ -1214,7 +1223,7 @@
     for t in range(half_blocks):
         write_out(t).wait()
         write_grad(t).wait()
-        send_dn1(t).wait_send()
+        send_out(t).wait_send()
     send_final(0, 0, early).wait_send()
     send_final(1, early, rows_final - early).wait()
     late = pl.ds(early, rows_final - early)
@@ -1235,14 +1244,18 @@
     chunks, _, _ = layout_of(width, width // 2, down.shape[1] // 2)
     block_out_ref[...] = block_out[...]
     input_grad_ref[...] = input_grad[...]
-    targets = {"query": query, "key": key, "value": value, "out": out, "gate": gate, "up": up, "down": down}
-    for name, target in targets.items():
+    half_pieces = width // LANES // 2
+    targets = (
+        ("query", query, 0), ("key", key, 0), ("value", value, 0), ("out", out, 0), ("down", down, 0),
+        ("gate0", gate, 0), ("gate1", gate, half_pieces), ("up0", up, 0), ("up1", up, half_pieces),
+    )
+    for name, target, skipped in targets:
         _, _, kind, pieces, each, at = chunks[name]
         half = each // 2
         for p in range(pieces):
             rows = pl.ds(at + p * half, half)
             if kind == "B":
-                target[:, p * LANES : (p + 1) * LANES] = final[taken, rows, :]
+                target[:, (skipped + p) * LANES : (skipped + p + 1) * LANES] = final[taken, rows, :]
             else:
                 for whose in range(2):
                     first = ((core if whose == 0 else 1 - core) * pieces + p) * LANES

time: 106 us -> 104 us (0.981)
  Pallas kernels: 105 us -> 103 us
    pallas_call x1, Pallas kernels: 102 us -> 99.4 us  [fused_shards(): pl.pallas_call(block_kernel, out_shape=(shape(half_tokens, width), shape(...]
where the time goes in v6:
time: 104 us; the launch traced here: 103 us
  Pallas kernels  103 us (99%)
    pallas_call x1, Pallas kernels, fused_shards(): pl.pallas_call(block_kernel, out_shape=(shape(half_tokens, width), shape(...  99.4 us
    pallas_call x1, Pallas kernels, fused_shards(): pl.pallas_call(hand_out, out_shape=outs, in_specs=[vmem] * 3, out_specs=[...  3.32 us

profile of v6, /device:TPU:0, one launch (start us, length us, event | category | flops | bytes accessed | tf_op | source)
XLA Modules:
  0.0 103.4 jit_solution(7406064522841855475)
XLA Ops:
  0.6 99.4 %block.1 = (bf16[512,768]{1,0:T(8,128)(2,1)}, bf16[512,768]{1,0:T(8,128)(2,1)}, f32[2,1488,128]{2,1,0:T(8,128)}) custom-call(bf16[512,768]{1,0:T(8,128)(2,1)} %bitcast.11, s32[1,512]{1,0:T(1,128)} %ids_hbm.1, bf16[512,768]{1,0:T(8,128)(2,1)} %bitcast.12, bf16[768,768]{1,0:T(8,128)(2,1)} %wq_hbm.1, bf16[768,768]{1,0:T(8,128)(2,1)} %wk_hbm.1, ...), custom_call_target="tpu_custom_call" | custom-call | tf_op jit(solution)/shard_map/block/pallas_call | solution.py:1303
  100.1 3.3 %hand_out.1 = (bf16[512,768]{1,0:T(8,128)(2,1)}, bf16[512,768]{1,0:T(8,128)(2,1)}, f32[24]{0:T(128)}, f32[24,768]{1,0:T(8,128)}, f32[24,768]{1,0:T(8,128)}, /*in...) custom-call(f32[2,1488,128]{2,1,0:T(8,128)} %get-tuple-element.25.fi, ...), custom_call_target="tpu_custom_call" | custom-call | tf_op jit(solution)/shard_map/hand_out/pallas_call | solution.py:1326
